TPU v7x, 1024 devices: a whole 8x8x8 slice. The times are simulated.
1024 devices in a mesh: lon: 64 (over z_hi, y, core), lat: 16 (over x, z_lo).
Axes of the slice: x: 8, y: 8, z: 8 (z_hi: 4, z_lo: 2; z = z_hi * 2 + z_lo), core: 2. Of those that a mesh axis runs over, the one named last changes fastest.
Arguments:
- depth_init: float32 [4096, 8192], P('lat', 'lon'), may hold values from 0.5 to 2.5
- ground: float32 [4096, 8192], P('lat', 'lon'), may hold values from -4 to 4
- roughness: float32 [4096, 8192], P('lat', 'lon'), may hold values from 0.02 to 0.12
- river_init: float32 [4096, 8192], P('lat', 'lon'), may hold values from 0.5 to 4.5
- reach_mask: int32 [4096, 64], P('lat', 'lon'), may hold values from 0 to 1, as said below
- width_class: int32 [4096, 8192], P('lat', 'lon'), may hold values from 0 to 7
- bank_class: int32 [4096, 8192], P('lat', 'lon'), may hold values from 0 to 7
Outputs:
- flood_depth: float32 [4096, 8192], P('lat', 'lon')
- river_depth: float32 [4096, 8192], P('lat', 'lon')
- flow_east: float32 [4096, 8192], P('lat', 'lon')
- flow_north: float32 [4096, 8192], P('lat', 'lon')
Inputs may be any that keep to these rules, and one draw needn't show every extreme that they name: Call the 256 rows of one lat index and one lon index of reach_mask a tile. A tile has at most 64 channelled reaches, and some tile exactly 64. A tile with more than 32 has 34 or more, and lies four or more lon indices (around the cycle) from any other such tile of the same lat index; every other tile has at most 16, and some tile beside a full one exactly that many.
All inputs are finite; a program needn't handle non-finite values.
Results may differ from a plain program's by a relative error of at most 0.00002.
Values sent between devices are 32-bit elements; how exact they have to be, the bound alone decides.
A program may use at most 32 MiB of HBM per device.

v0:
```python
import jax
import jax.numpy as jnp
from jax import lax
from jax.sharding import PartitionSpec as P

SUB = 8
STEPS = 4


GRAVITY = 9.81
CELL_SIZE = 90.0
TIME_STEP = 10.0
SHALLOW = 0.1
EXCHANGE = 0.01
CHANNEL_MANNING = 0.035


def padded(block, sides, width, periodic):
    for axis, dim in sides:
        count = lax.axis_size(axis)
        forward = [(i, i + 1) for i in range(count - 1)]
        if periodic:
            forward.append((count - 1, 0))
        backward = [(target, source) for source, target in forward]
        low = lax.ppermute(
            lax.slice_in_dim(block, block.shape[dim] - width, None, axis=dim), axis, forward
        )
        high = lax.ppermute(lax.slice_in_dim(block, 0, width, axis=dim), axis, backward)
        block = jnp.concatenate([low, block, high], axis=dim)
    return block


def face_flow(
    current, surface_from, surface_to, ground_from, ground_to, friction, breadth, duration
):
    height = jnp.maximum(surface_from, surface_to) - jnp.maximum(ground_from, ground_to)
    driven = (
        current - GRAVITY * duration * breadth * height * (surface_to - surface_from) / CELL_SIZE
    )
    resisted = 1.0 + GRAVITY * duration * friction * jnp.abs(current) / (
        height * height + SHALLOW * SHALLOW
    ) ** (7.0 / 6.0)
    return driven / resisted


def reach_update(river_bed, channel_width, safe_width, river_depth, discharge, surface):
    duration = TIME_STEP / SUB
    breadth = 0.5 * (channel_width[:, :-1] + channel_width[:, 1:])
    safe_breadth = 0.5 * (safe_width[:, :-1] + safe_width[:, 1:])
    friction = CHANNEL_MANNING * CHANNEL_MANNING / safe_breadth
    closed = jnp.zeros_like(river_depth[:, :1])
    gathered = jnp.zeros_like(river_depth)
    for substep in range(SUB):
        water_level = river_bed + river_depth
        interior = face_flow(
            discharge[:, :-1],
            water_level[:, :-1],
            water_level[:, 1:],
            river_bed[:, :-1],
            river_bed[:, 1:],
            friction,
            breadth,
            duration,
        )
        discharge = jnp.concatenate([interior, closed], axis=1)
        inflow = jnp.concatenate([closed, interior], axis=1)
        transfer = EXCHANGE * (water_level - surface)
        river_depth = river_depth + duration * (
            (inflow - discharge) / (safe_width * CELL_SIZE) - transfer
        )
        gathered = gathered + duration * transfer
    return (river_depth, discharge, gathered)


def channel_slots(slot_state):
    safe_width = jnp.where(slot_state[1] > 0.0, slot_state[1], 1.0)
    new_river, new_discharge, gathered = reach_update(
        slot_state[0], slot_state[1], safe_width, slot_state[2], slot_state[3], slot_state[4]
    )
    return jnp.stack([new_river, new_discharge, gathered])


def rims(fields):
    across = padded(fields, (("lon", 2),), 1, True)
    along_lat = padded(fields, (("lat", 1),), 1, False)
    return (across, along_lat)


def body(depth_init, ground, roughness, river_init, reach_mask, width_class, bank_class):
    row_count, col_count = ground.shape
    most_slots = row_count // 4
    channel_width = 8.0 + 9.0 * width_class.astype(jnp.float32)
    river_bed = ground - (1.0 + 0.5 * bank_class.astype(jnp.float32))
    lat_number = lax.axis_index("lat")
    lat_total = lax.axis_size("lat")
    row_numbers = jnp.arange(row_count)
    open_north = ((row_numbers < row_count - 1) | (lat_number < lat_total - 1))[:, None]
    open_south = lat_number > 0
    static_across, static_along = rims(jnp.stack([ground, roughness]))
    ground_east = static_across[0, :, 2:]
    rough_east = static_across[1, :, 2:]
    ground_west = static_across[0, :, 0]
    rough_west = static_across[1, :, 0]
    ground_north = static_along[0, 2:, :]
    rough_north = static_along[1, 2:, :]
    ground_south = static_along[0, 0, :]
    rough_south = static_along[1, 0, :]
    channelled = reach_mask[:, 0] > 0
    channel_count = jnp.sum(channelled.astype(jnp.int32))
    listed = jnp.nonzero(channelled, size=most_slots, fill_value=0)[0].astype(jnp.int32)
    positions = jnp.arange(most_slots)
    occupied = positions < channel_count
    chosen_rows = listed[jnp.clip(positions, 0, most_slots - 1)]
    target = jnp.where(occupied, chosen_rows, row_count).astype(jnp.int32)

    def select_rows(field):
        return jnp.where(occupied[:, None], field[chosen_rows], 0.0)

    slot_bed = select_rows(river_bed)
    slot_width = select_rows(channel_width)
    flood = depth_init
    river_depth = river_init
    discharge = jnp.zeros((row_count, col_count), jnp.float32)
    flow_east = jnp.zeros((row_count, col_count), jnp.float32)
    flow_north = jnp.zeros((row_count, col_count), jnp.float32)
    flow_west = jnp.zeros((row_count,), jnp.float32)
    flow_south = jnp.zeros((col_count,), jnp.float32)
    for repeat in range(STEPS):
        depth_across, depth_along = rims(flood[None])
        surface = ground + flood
        surface_east = ground_east + depth_across[0, :, 2:]
        surface_west = ground_west + depth_across[0, :, 0]
        surface_north = ground_north + depth_along[0, 2:, :]
        surface_south = ground_south + depth_along[0, 0, :]
        flow_east = face_flow(
            flow_east,
            surface,
            surface_east,
            ground,
            ground_east,
            roughness * rough_east,
            1.0,
            TIME_STEP,
        )
        flow_west = face_flow(
            flow_west,
            surface_west,
            surface[:, 0],
            ground_west,
            ground[:, 0],
            rough_west * roughness[:, 0],
            1.0,
            TIME_STEP,
        )
        north_flux = face_flow(
            flow_north,
            surface,
            surface_north,
            ground,
            ground_north,
            roughness * rough_north,
            1.0,
            TIME_STEP,
        )
        flow_north = jnp.where(open_north, north_flux, 0.0)
        south_flux = face_flow(
            flow_south,
            surface_south,
            surface[0],
            ground_south,
            ground[0],
            rough_south * roughness[0],
            1.0,
            TIME_STEP,
        )
        flow_south = jnp.where(open_south, south_flux, 0.0)
        from_west = jnp.concatenate([flow_west[:, None], flow_east[:, :-1]], axis=1)
        from_south = jnp.concatenate([flow_south[None, :], flow_north[:-1]], axis=0)
        flooded = flood + TIME_STEP / CELL_SIZE * (from_west - flow_east + from_south - flow_north)
        slot_state = jnp.stack(
            [
                slot_bed,
                slot_width,
                select_rows(river_depth),
                select_rows(discharge),
                select_rows(surface),
            ]
        )
        results = channel_slots(slot_state)
        river_depth = river_depth.at[target].set(results[0], mode="drop")
        discharge = discharge.at[target].set(results[1], mode="drop")
        gathered = jnp.zeros_like(flood).at[target].set(results[2], mode="drop")
        flood = flooded + jnp.where(channelled[:, None], gathered * channel_width / CELL_SIZE, 0.0)
    return (flood, river_depth, flow_east, flow_north)


def solution(mesh):
    return jax.shard_map(
        body,
        mesh=mesh,
        in_specs=(
            P("lat", "lon"),
            P("lat", "lon"),
            P("lat", "lon"),
            P("lat", "lon"),
            P("lat", "lon"),
            P("lat", "lon"),
            P("lat", "lon"),
        ),
        out_specs=(P("lat", "lon"), P("lat", "lon"), P("lat", "lon"), P("lat", "lon")),
        check_vma=False,
    )
```

profile of v0, /device:TPU:134, one launch (start us, length us, event | category | flops | bytes accessed | tf_op | source)
XLA Modules:
  0.0 134.6 jit_solution(10979483410869257663)
XLA Ops:
  0.6 0.9 copy.196
  1.7 18.8 %collective-permute-start.3 = (f32[1,256,1]{1,2,0:T(1,128)S(1)}, f32[1,256,1]{1,2,0:T(1,128)S(1)}, u32[]{:S(2)}, u32[]{:S(2)}) collective-permute-start(f32[1,256,1]{1,2,0:T(1,128)S(1)} %get-tuple-element.93), channel_id=1, source_target_pairs={{16,0},{32,16},{48,32},{64,48},{80,64},{96,80},{112,96},{128,112},... | collective-permute-start | bytes 3080 | tf_op jit(solution)/shard_map/ppermute | solution.py:28
  20.7 2.6 %collective-permute-start.2 = (f32[2,256,1]{1,2,0:T(1,128)S(1)}, f32[2,256,1]{1,2,0:T(1,128)S(1)}, u32[]{:S(2)}, u32[]{:S(2)}) collective-permute-start(f32[2,256,1]{1,2,0:T(1,128)S(1)} %get-tuple-element.76), channel_id=1, source_target_pairs={{16,0},{32,16},{48,32},{64,48},{80,64},{96,80},{112,96},{128,112},... | collective-permute-start | bytes 6152 | tf_op jit(solution)/shard_map/ppermute | solution.py:28
  23.4 1.9 %collective-permute-start.7 = (f32[1,1,128]{1,2,0:T(8,128)S(1)}, f32[1,1,128]{1,2,0:T(8,128)S(1)}, u32[]{:S(2)}, u32[]{:S(2)}) collective-permute-start(f32[1,1,128]{1,2,0:T(8,128)S(1)} %get-tuple-element.91), channel_id=1, source_target_pairs={{1,0},{2,1},{3,2},{4,3},{5,4},{6,5},{7,6},{8,7},{9,8},{10,9},{11,1... | collective-permute-start | bytes 1544 | tf_op jit(solution)/shard_map/ppermute | solution.py:28
  25.4 3.9 %collective-permute-start.6 = (f32[2,1,128]{1,2,0:T(8,128)S(1)}, f32[2,1,128]{1,2,0:T(8,128)S(1)}, u32[]{:S(2)}, u32[]{:S(2)}) collective-permute-start(f32[2,1,128]{1,2,0:T(8,128)S(1)} %get-tuple-element.74), channel_id=1, source_target_pairs={{1,0},{2,1},{3,2},{4,3},{5,4},{6,5},{7,6},{8,7},{9,8},{10,9},{11,1... | collective-permute-start | bytes 3080 | tf_op jit(solution)/shard_map/ppermute | solution.py:28
  29.3 1.9 %collective-permute-start.1 = (f32[1,256,1]{1,2,0:T(1,128)S(1)}, f32[1,256,1]{1,2,0:T(1,128)S(1)}, u32[]{:S(2)}, u32[]{:S(2)}) collective-permute-start(f32[1,256,1]{1,2,0:T(1,128)S(1)} %get-tuple-element.92), channel_id=1, source_target_pairs={{0,16},{16,32},{32,48},{48,64},{64,80},{80,96},{96,112},{112,128},... | collective-permute-start | bytes 3080 | tf_op jit(solution)/shard_map/ppermute | solution.py:25
  31.3 0.6 fusion.148
  32.6 2.3 %scatter_custom_fusion = s32[64]{0:T(128)S(1)} fusion(s32[256]{0:T(256)S(1)} %bitcast.195, s32[256]{0:T(256)S(1)} %broadcast.723, s32[]{:T(128)} %constant.236.clone.1), kind=kCustom, calls=%fused_computation.353 | custom fusion | flops 256 | bytes 260 | tf_op jit(solution)/shard_map/scatter-add | solution.py:110
  35.2 0.7 iota_compare_fusion
  35.9 0.7 compare_select_fusion.7
  36.6 0.8 gather_fusion
  37.3 0.7 fusion.144
  38.2 0.8 copy-done.5
  40.5 0.6 gather_fusion.5
  42.3 1.9 %collective-permute-start = (f32[2,256,1]{1,2,0:T(1,128)S(1)}, f32[2,256,1]{1,2,0:T(1,128)S(1)}, u32[]{:S(2)}, u32[]{:S(2)}) collective-permute-start(f32[2,256,1]{1,2,0:T(1,128)S(1)} %get-tuple-element.75), channel_id=1, source_target_pairs={{0,16},{16,32},{32,48},{48,64},{64,80},{80,96},{96,112},{112,128},... | collective-permute-start | bytes 6152 | tf_op jit(solution)/shard_map/ppermute | solution.py:25
  44.3 4.1 %collective-permute-start.5 = (f32[1,1,128]{1,2,0:T(8,128)S(1)}, f32[1,1,128]{1,2,0:T(8,128)S(1)}, u32[]{:S(2)}, u32[]{:S(2)}) collective-permute-start(f32[1,1,128]{1,2,0:T(8,128)S(1)} %get-tuple-element.90), channel_id=1, source_target_pairs={{0,1},{1,2},{2,3},{3,4},{4,5},{5,6},{6,7},{7,8},{8,9},{9,10},{10,1... | collective-permute-start | bytes 1544 | tf_op jit(solution)/shard_map/ppermute | solution.py:25
  48.7 3.9 %collective-permute-start.4 = (f32[2,1,128]{1,2,0:T(8,128)S(1)}, f32[2,1,128]{1,2,0:T(8,128)S(1)}, u32[]{:S(2)}, u32[]{:S(2)}) collective-permute-start(f32[2,1,128]{1,2,0:T(8,128)S(1)} %get-tuple-element.73), channel_id=1, source_target_pairs={{0,1},{1,2},{2,3},{3,4},{4,5},{5,6},{6,7},{7,8},{8,9},{9,10},{10,1... | collective-permute-start | bytes 3080 | tf_op jit(solution)/shard_map/ppermute | solution.py:25
  53.0 0.6 gather_fusion.1
  55.9 0.9 scatter_custom_fusion.1
  57.3 7.3 %collective-permute-start.9 = (f32[1,256,1]{1,2,0:T(1,128)S(1)}, f32[1,256,1]{1,2,0:T(1,128)S(1)}, u32[]{:S(2)}, u32[]{:S(2)}) collective-permute-start(f32[1,256,1]{1,2,0:T(1,128)S(1)} %get-tuple-element.88), channel_id=1, source_target_pairs={{16,0},{32,16},{48,32},{64,48},{80,64},{96,80},{112,96},{128,112},... | collective-permute-start | bytes 3080 | tf_op jit(solution)/shard_map/ppermute | solution.py:28
  64.6 1.9 %collective-permute-start.11 = (f32[1,1,128]{1,2,0:T(8,128)S(1)}, f32[1,1,128]{1,2,0:T(8,128)S(1)}, u32[]{:S(2)}, u32[]{:S(2)}) collective-permute-start(f32[1,1,128]{1,2,0:T(8,128)S(1)} %get-tuple-element.86), channel_id=1, source_target_pairs={{1,0},{2,1},{3,2},{4,3},{5,4},{6,5},{7,6},{8,7},{9,8},{10,9},{11,1... | collective-permute-start | bytes 1544 | tf_op jit(solution)/shard_map/ppermute | solution.py:28
  66.5 1.9 %collective-permute-start.8 = (f32[1,256,1]{1,2,0:T(1,128)S(1)}, f32[1,256,1]{1,2,0:T(1,128)S(1)}, u32[]{:S(2)}, u32[]{:S(2)}) collective-permute-start(f32[1,256,1]{1,2,0:T(1,128)S(1)} %get-tuple-element.87), channel_id=1, source_target_pairs={{0,16},{16,32},{32,48},{48,64},{64,80},{80,96},{96,112},{112,128},... | collective-permute-start | bytes 3080 | tf_op jit(solution)/shard_map/ppermute | solution.py:25
  68.5 6.0 %collective-permute-start.10 = (f32[1,1,128]{1,2,0:T(8,128)S(1)}, f32[1,1,128]{1,2,0:T(8,128)S(1)}, u32[]{:S(2)}, u32[]{:S(2)}) collective-permute-start(f32[1,1,128]{1,2,0:T(8,128)S(1)} %get-tuple-element.85), channel_id=1, source_target_pairs={{0,1},{1,2},{2,3},{3,4},{4,5},{5,6},{6,7},{7,8},{8,9},{9,10},{10,1... | collective-permute-start | bytes 1544 | tf_op jit(solution)/shard_map/ppermute | solution.py:25
  74.5 0.8 scatter_custom_fusion.3
  75.3 0.9 scatter_custom_fusion.2
  77.9 0.6 gather_fusion.7
  80.0 0.9 scatter_custom_fusion.4
  81.6 7.6 %collective-permute-start.13 = (f32[1,256,1]{1,2,0:T(1,128)S(1)}, f32[1,256,1]{1,2,0:T(1,128)S(1)}, u32[]{:S(2)}, u32[]{:S(2)}) collective-permute-start(f32[1,256,1]{1,2,0:T(1,128)S(1)} %get-tuple-element.84), channel_id=1, source_target_pairs={{16,0},{32,16},{48,32},{64,48},{80,64},{96,80},{112,96},{128,112},... | collective-permute-start | bytes 3080 | tf_op jit(solution)/shard_map/ppermute | solution.py:28
  89.2 1.9 %collective-permute-start.15 = (f32[1,1,128]{1,2,0:T(8,128)S(1)}, f32[1,1,128]{1,2,0:T(8,128)S(1)}, u32[]{:S(2)}, u32[]{:S(2)}) collective-permute-start(f32[1,1,128]{1,2,0:T(8,128)S(1)} %get-tuple-element.82), channel_id=1, source_target_pairs={{1,0},{2,1},{3,2},{4,3},{5,4},{6,5},{7,6},{8,7},{9,8},{10,9},{11,1... | collective-permute-start | bytes 1544 | tf_op jit(solution)/shard_map/ppermute | solution.py:28
  91.1 1.9 %collective-permute-start.12 = (f32[1,256,1]{1,2,0:T(1,128)S(1)}, f32[1,256,1]{1,2,0:T(1,128)S(1)}, u32[]{:S(2)}, u32[]{:S(2)}) collective-permute-start(f32[1,256,1]{1,2,0:T(1,128)S(1)} %get-tuple-element.83), channel_id=1, source_target_pairs={{0,16},{16,32},{32,48},{48,64},{64,80},{80,96},{96,112},{112,128},... | collective-permute-start | bytes 3080 | tf_op jit(solution)/shard_map/ppermute | solution.py:25
  93.0 6.0 %collective-permute-start.14 = (f32[1,1,128]{1,2,0:T(8,128)S(1)}, f32[1,1,128]{1,2,0:T(8,128)S(1)}, u32[]{:S(2)}, u32[]{:S(2)}) collective-permute-start(f32[1,1,128]{1,2,0:T(8,128)S(1)} %get-tuple-element.81), channel_id=1, source_target_pairs={{0,1},{1,2},{2,3},{3,4},{4,5},{5,6},{6,7},{7,8},{8,9},{9,10},{10,1... | collective-permute-start | bytes 1544 | tf_op jit(solution)/shard_map/ppermute | solution.py:25
  99.1 0.8 scatter_custom_fusion.6
  99.9 0.9 scatter_custom_fusion.5
  102.5 0.6 gather_fusion.10
  104.8 0.9 scatter_custom_fusion.7
  106.2 7.6 %collective-permute-start.17 = (f32[1,256,1]{1,2,0:T(1,128)S(1)}, f32[1,256,1]{1,2,0:T(1,128)S(1)}, u32[]{:S(2)}, u32[]{:S(2)}) collective-permute-start(f32[1,256,1]{1,2,0:T(1,128)S(1)} %get-tuple-element.80), channel_id=1, source_target_pairs={{16,0},{32,16},{48,32},{64,48},{80,64},{96,80},{112,96},{128,112},... | collective-permute-start | bytes 3080 | tf_op jit(solution)/shard_map/ppermute | solution.py:28
  113.8 1.9 %collective-permute-start.19 = (f32[1,1,128]{1,2,0:T(8,128)S(1)}, f32[1,1,128]{1,2,0:T(8,128)S(1)}, u32[]{:S(2)}, u32[]{:S(2)}) collective-permute-start(f32[1,1,128]{1,2,0:T(8,128)S(1)} %get-tuple-element.78), channel_id=1, source_target_pairs={{1,0},{2,1},{3,2},{4,3},{5,4},{6,5},{7,6},{8,7},{9,8},{10,9},{11,1... | collective-permute-start | bytes 1544 | tf_op jit(solution)/shard_map/ppermute | solution.py:28
  115.8 1.9 %collective-permute-start.16 = (f32[1,256,1]{1,2,0:T(1,128)S(1)}, f32[1,256,1]{1,2,0:T(1,128)S(1)}, u32[]{:S(2)}, u32[]{:S(2)}) collective-permute-start(f32[1,256,1]{1,2,0:T(1,128)S(1)} %get-tuple-element.79), channel_id=1, source_target_pairs={{0,16},{16,32},{32,48},{48,64},{64,80},{80,96},{96,112},{112,128},... | collective-permute-start | bytes 3080 | tf_op jit(solution)/shard_map/ppermute | solution.py:25
  117.7 6.0 %collective-permute-start.18 = (f32[1,1,128]{1,2,0:T(8,128)S(1)}, f32[1,1,128]{1,2,0:T(8,128)S(1)}, u32[]{:S(2)}, u32[]{:S(2)}) collective-permute-start(f32[1,1,128]{1,2,0:T(8,128)S(1)} %get-tuple-element.77), channel_id=1, source_target_pairs={{0,1},{1,2},{2,3},{3,4},{4,5},{5,6},{6,7},{7,8},{8,9},{9,10},{10,1... | collective-permute-start | bytes 1544 | tf_op jit(solution)/shard_map/ppermute | solution.py:25
  123.7 0.8 scatter_custom_fusion.9
  124.6 0.9 scatter_custom_fusion.8
  127.1 0.6 gather_fusion.13
  129.6 0.9 scatter_custom_fusion.10
  130.6 0.8 copy.123
  131.3 0.8 copy.124
  132.3 0.8 copy.122
  133.0 0.9 scatter_custom_fusion.11
  133.9 0.6 copy-done
  (173 shorter events, 18.7 us)
Async XLA Ops:
  0.6 1.0 copy-start.1
  1.6 18.9 %copy-start.3 = (f32[256,128]{1,0:T(8,128)S(1)}, f32[256,128]{1,0:T(8,128)}, u32[]{:S(2)}) copy-start(f32[256,128]{1,0:T(8,128)} %param.8) | copy-start | bytes 393220
  1.7 18.9 %copy-start.4 = (f32[256,128]{1,0:T(8,128)S(1)}, f32[256,128]{1,0:T(8,128)}, u32[]{:S(2)}) copy-start(f32[256,128]{1,0:T(8,128)} %param.9) | copy-start | bytes 393220
  1.7 40.6 %collective-permute-start.3 = (f32[1,256,1]{1,2,0:T(1,128)S(1)}, f32[1,256,1]{1,2,0:T(1,128)S(1)}, u32[]{:S(2)}, u32[]{:S(2)}) collective-permute-start(f32[1,256,1]{1,2,0:T(1,128)S(1)} %get-tuple-element.93), channel_id=1, source_target_pairs={{16,0},{32,16},{48,32},{64,48},{80,64},{96,80},{112,96},{128,112},... | collective-permute-start | bytes 3080 | tf_op jit(solution)/shard_map/ppermute | solution.py:28
  20.7 23.5 %collective-permute-start.2 = (f32[2,256,1]{1,2,0:T(1,128)S(1)}, f32[2,256,1]{1,2,0:T(1,128)S(1)}, u32[]{:S(2)}, u32[]{:S(2)}) collective-permute-start(f32[2,256,1]{1,2,0:T(1,128)S(1)} %get-tuple-element.76), channel_id=1, source_target_pairs={{16,0},{32,16},{48,32},{64,48},{80,64},{96,80},{112,96},{128,112},... | collective-permute-start | bytes 6152 | tf_op jit(solution)/shard_map/ppermute | solution.py:28
  23.4 25.2 %collective-permute-start.7 = (f32[1,1,128]{1,2,0:T(8,128)S(1)}, f32[1,1,128]{1,2,0:T(8,128)S(1)}, u32[]{:S(2)}, u32[]{:S(2)}) collective-permute-start(f32[1,1,128]{1,2,0:T(8,128)S(1)} %get-tuple-element.91), channel_id=1, source_target_pairs={{1,0},{2,1},{3,2},{4,3},{5,4},{6,5},{7,6},{8,7},{9,8},{10,9},{11,1... | collective-permute-start | bytes 1544 | tf_op jit(solution)/shard_map/ppermute | solution.py:28
  25.4 27.2 %collective-permute-start.6 = (f32[2,1,128]{1,2,0:T(8,128)S(1)}, f32[2,1,128]{1,2,0:T(8,128)S(1)}, u32[]{:S(2)}, u32[]{:S(2)}) collective-permute-start(f32[2,1,128]{1,2,0:T(8,128)S(1)} %get-tuple-element.74), channel_id=1, source_target_pairs={{1,0},{2,1},{3,2},{4,3},{5,4},{6,5},{7,6},{8,7},{9,8},{10,9},{11,1... | collective-permute-start | bytes 3080 | tf_op jit(solution)/shard_map/ppermute | solution.py:28
  29.3 1.9 %copy-start.6 = (s32[256,1]{0,1:T(1,128)S(1)}, s32[256,1]{0,1:T(1,128)}, u32[]{:S(2)}) copy-start(s32[256,1]{0,1:T(1,128)} %param.11) | copy-start | bytes 3076
  29.3 26.5 %collective-permute-start.1 = (f32[1,256,1]{1,2,0:T(1,128)S(1)}, f32[1,256,1]{1,2,0:T(1,128)S(1)}, u32[]{:S(2)}, u32[]{:S(2)}) collective-permute-start(f32[1,256,1]{1,2,0:T(1,128)S(1)} %get-tuple-element.92), channel_id=1, source_target_pairs={{0,16},{16,32},{32,48},{48,64},{64,80},{80,96},{96,112},{112,128},... | collective-permute-start | bytes 3080 | tf_op jit(solution)/shard_map/ppermute | solution.py:25
  36.5 1.5 %copy-start.2 = (s32[256,128]{1,0:T(8,128)S(1)}, s32[256,128]{1,0:T(8,128)}, u32[]{:S(2)}) copy-start(s32[256,128]{1,0:T(8,128)} %param.12) | copy-start | bytes 393220
  38.1 0.9 copy-start.5
  39.0 0.7 slice-start
  39.7 0.7 slice-start.1
  42.3 13.5 %collective-permute-start = (f32[2,256,1]{1,2,0:T(1,128)S(1)}, f32[2,256,1]{1,2,0:T(1,128)S(1)}, u32[]{:S(2)}, u32[]{:S(2)}) collective-permute-start(f32[2,256,1]{1,2,0:T(1,128)S(1)} %get-tuple-element.75), channel_id=1, source_target_pairs={{0,16},{16,32},{32,48},{48,64},{64,80},{80,96},{96,112},{112,128},... | collective-permute-start | bytes 6152 | tf_op jit(solution)/shard_map/ppermute | solution.py:25
  44.3 12.5 %collective-permute-start.5 = (f32[1,1,128]{1,2,0:T(8,128)S(1)}, f32[1,1,128]{1,2,0:T(8,128)S(1)}, u32[]{:S(2)}, u32[]{:S(2)}) collective-permute-start(f32[1,1,128]{1,2,0:T(8,128)S(1)} %get-tuple-element.90), channel_id=1, source_target_pairs={{0,1},{1,2},{2,3},{3,4},{4,5},{5,6},{6,7},{7,8},{8,9},{9,10},{10,1... | collective-permute-start | bytes 1544 | tf_op jit(solution)/shard_map/ppermute | solution.py:25
  48.7 8.2 %collective-permute-start.4 = (f32[2,1,128]{1,2,0:T(8,128)S(1)}, f32[2,1,128]{1,2,0:T(8,128)S(1)}, u32[]{:S(2)}, u32[]{:S(2)}) collective-permute-start(f32[2,1,128]{1,2,0:T(8,128)S(1)} %get-tuple-element.73), channel_id=1, source_target_pairs={{0,1},{1,2},{2,3},{3,4},{4,5},{5,6},{6,7},{7,8},{8,9},{9,10},{10,1... | collective-permute-start | bytes 3080 | tf_op jit(solution)/shard_map/ppermute | solution.py:25
  57.3 20.3 %collective-permute-start.9 = (f32[1,256,1]{1,2,0:T(1,128)S(1)}, f32[1,256,1]{1,2,0:T(1,128)S(1)}, u32[]{:S(2)}, u32[]{:S(2)}) collective-permute-start(f32[1,256,1]{1,2,0:T(1,128)S(1)} %get-tuple-element.88), channel_id=1, source_target_pairs={{16,0},{32,16},{48,32},{64,48},{80,64},{96,80},{112,96},{128,112},... | collective-permute-start | bytes 3080 | tf_op jit(solution)/shard_map/ppermute | solution.py:28
  64.6 16.4 %collective-permute-start.11 = (f32[1,1,128]{1,2,0:T(8,128)S(1)}, f32[1,1,128]{1,2,0:T(8,128)S(1)}, u32[]{:S(2)}, u32[]{:S(2)}) collective-permute-start(f32[1,1,128]{1,2,0:T(8,128)S(1)} %get-tuple-element.86), channel_id=1, source_target_pairs={{1,0},{2,1},{3,2},{4,3},{5,4},{6,5},{7,6},{8,7},{9,8},{10,9},{11,1... | collective-permute-start | bytes 1544 | tf_op jit(solution)/shard_map/ppermute | solution.py:28
  66.5 13.5 %collective-permute-start.8 = (f32[1,256,1]{1,2,0:T(1,128)S(1)}, f32[1,256,1]{1,2,0:T(1,128)S(1)}, u32[]{:S(2)}, u32[]{:S(2)}) collective-permute-start(f32[1,256,1]{1,2,0:T(1,128)S(1)} %get-tuple-element.87), channel_id=1, source_target_pairs={{0,16},{16,32},{32,48},{48,64},{64,80},{80,96},{96,112},{112,128},... | collective-permute-start | bytes 3080 | tf_op jit(solution)/shard_map/ppermute | solution.py:25
  68.5 11.3 %collective-permute-start.10 = (f32[1,1,128]{1,2,0:T(8,128)S(1)}, f32[1,1,128]{1,2,0:T(8,128)S(1)}, u32[]{:S(2)}, u32[]{:S(2)}) collective-permute-start(f32[1,1,128]{1,2,0:T(8,128)S(1)} %get-tuple-element.85), channel_id=1, source_target_pairs={{0,1},{1,2},{2,3},{3,4},{4,5},{5,6},{6,7},{7,8},{8,9},{9,10},{10,1... | collective-permute-start | bytes 1544 | tf_op jit(solution)/shard_map/ppermute | solution.py:25
  81.6 20.6 %collective-permute-start.13 = (f32[1,256,1]{1,2,0:T(1,128)S(1)}, f32[1,256,1]{1,2,0:T(1,128)S(1)}, u32[]{:S(2)}, u32[]{:S(2)}) collective-permute-start(f32[1,256,1]{1,2,0:T(1,128)S(1)} %get-tuple-element.84), channel_id=1, source_target_pairs={{16,0},{32,16},{48,32},{64,48},{80,64},{96,80},{112,96},{128,112},... | collective-permute-start | bytes 3080 | tf_op jit(solution)/shard_map/ppermute | solution.py:28
  89.2 15.2 %collective-permute-start.15 = (f32[1,1,128]{1,2,0:T(8,128)S(1)}, f32[1,1,128]{1,2,0:T(8,128)S(1)}, u32[]{:S(2)}, u32[]{:S(2)}) collective-permute-start(f32[1,1,128]{1,2,0:T(8,128)S(1)} %get-tuple-element.82), channel_id=1, source_target_pairs={{1,0},{2,1},{3,2},{4,3},{5,4},{6,5},{7,6},{8,7},{9,8},{10,9},{11,1... | collective-permute-start | bytes 1544 | tf_op jit(solution)/shard_map/ppermute | solution.py:28
  91.1 13.7 %collective-permute-start.12 = (f32[1,256,1]{1,2,0:T(1,128)S(1)}, f32[1,256,1]{1,2,0:T(1,128)S(1)}, u32[]{:S(2)}, u32[]{:S(2)}) collective-permute-start(f32[1,256,1]{1,2,0:T(1,128)S(1)} %get-tuple-element.83), channel_id=1, source_target_pairs={{0,16},{16,32},{32,48},{48,64},{64,80},{80,96},{96,112},{112,128},... | collective-permute-start | bytes 3080 | tf_op jit(solution)/shard_map/ppermute | solution.py:25
  93.0 12.8 %collective-permute-start.14 = (f32[1,1,128]{1,2,0:T(8,128)S(1)}, f32[1,1,128]{1,2,0:T(8,128)S(1)}, u32[]{:S(2)}, u32[]{:S(2)}) collective-permute-start(f32[1,1,128]{1,2,0:T(8,128)S(1)} %get-tuple-element.81), channel_id=1, source_target_pairs={{0,1},{1,2},{2,3},{3,4},{4,5},{5,6},{6,7},{7,8},{8,9},{9,10},{10,1... | collective-permute-start | bytes 1544 | tf_op jit(solution)/shard_map/ppermute | solution.py:25
  106.2 20.6 %collective-permute-start.17 = (f32[1,256,1]{1,2,0:T(1,128)S(1)}, f32[1,256,1]{1,2,0:T(1,128)S(1)}, u32[]{:S(2)}, u32[]{:S(2)}) collective-permute-start(f32[1,256,1]{1,2,0:T(1,128)S(1)} %get-tuple-element.80), channel_id=1, source_target_pairs={{16,0},{32,16},{48,32},{64,48},{80,64},{96,80},{112,96},{128,112},... | collective-permute-start | bytes 3080 | tf_op jit(solution)/shard_map/ppermute | solution.py:28
  113.8 15.4 %collective-permute-start.19 = (f32[1,1,128]{1,2,0:T(8,128)S(1)}, f32[1,1,128]{1,2,0:T(8,128)S(1)}, u32[]{:S(2)}, u32[]{:S(2)}) collective-permute-start(f32[1,1,128]{1,2,0:T(8,128)S(1)} %get-tuple-element.78), channel_id=1, source_target_pairs={{1,0},{2,1},{3,2},{4,3},{5,4},{6,5},{7,6},{8,7},{9,8},{10,9},{11,1... | collective-permute-start | bytes 1544 | tf_op jit(solution)/shard_map/ppermute | solution.py:28
  115.8 13.8 %collective-permute-start.16 = (f32[1,256,1]{1,2,0:T(1,128)S(1)}, f32[1,256,1]{1,2,0:T(1,128)S(1)}, u32[]{:S(2)}, u32[]{:S(2)}) collective-permute-start(f32[1,256,1]{1,2,0:T(1,128)S(1)} %get-tuple-element.79), channel_id=1, source_target_pairs={{0,16},{16,32},{32,48},{48,64},{64,80},{80,96},{96,112},{112,128},... | collective-permute-start | bytes 3080 | tf_op jit(solution)/shard_map/ppermute | solution.py:25
  117.7 14.4 %collective-permute-start.18 = (f32[1,1,128]{1,2,0:T(8,128)S(1)}, f32[1,1,128]{1,2,0:T(8,128)S(1)}, u32[]{:S(2)}, u32[]{:S(2)}) collective-permute-start(f32[1,1,128]{1,2,0:T(8,128)S(1)} %get-tuple-element.77), channel_id=1, source_target_pairs={{0,1},{1,2},{2,3},{3,4},{4,5},{5,6},{6,7},{7,8},{8,9},{9,10},{10,1... | collective-permute-start | bytes 1544 | tf_op jit(solution)/shard_map/ppermute | solution.py:25
  133.9 0.7 copy-start
where the time goes:
time: 135 us
  starting transfers between devices  91.1 us (67%)
  other arithmetic  21.9 us (16%)
  local copies, waits for them, and re-layouts  19.7 us (15%)
  between operations  1.87 us (1%)
    ppermute x10, starting transfers between devices, padded(): lax.ppermute(lax.slice_in_dim(block, 0, width, axis=dim), axis, backward)  55.4 us
    ppermute x10, starting transfers between devices, padded(): lax.ppermute(lax.slice_in_dim(block, block.shape[dim] - width, None, axis...  35.7 us
    gather x14, local copies, waits for them, and re-layouts, select_rows(): return jnp.where(occupied[:, None], field[chosen_rows], 0.0)  8.39 us
    unnamed x23, local copies, waits for them, and re-layouts  5.21 us
    div x40, other arithmetic, face_flow(): return driven / resisted  4.43 us
    scatter x4, other arithmetic, body(): river_depth = river_depth.at[target].set(results[0], mode='drop')  3.62 us
    scatter x4, other arithmetic, body(): gathered = jnp.zeros_like(flood).at[target].set(results[2], mode='drop')  3.47 us
    add x31, other arithmetic, reach_update(): water_level = river_bed + river_depth  2.88 us
  transfers between devices with their start and end apart: 20, of which 0 were waited for; matrix products, arithmetic and copies ran while one was open for 26% of the time, Pallas kernels for 0%

commit v1 on v0

v1 whole, which is shorter than its diff:
```python
import functools
import math

import jax
import jax.numpy as jnp
from jax import lax
from jax.experimental import pallas as pl
from jax.experimental.pallas import tpu as pltpu
from jax.sharding import PartitionSpec as P

MESH = pl.DeviceIdType.MESH
F32 = jnp.float32
SUB = 8
STEPS = 4
ROWS = 256
COLS = 128
HALO = 24
WIDE = COLS + 2 * HALO
SEG = WIDE // 8
LANES = 128
TILES = 3
DEPTH, GROUND, ROUGH, RIVER, WIDTH, BED = range(6)
FROM_S, FROM_N, FROM_SW, FROM_SE, FROM_NW, FROM_NE = range(6)

GRAVITY = 9.81
CELL_SIZE = 90.0
TIME_STEP = 10.0
SHALLOW = 0.1
EXCHANGE = 0.01
CHANNEL_MANNING = 0.035
SHORT_STEP = TIME_STEP / SUB
POWER = -7.0 / 6.0 / math.log(2.0)


def exchange_kernel(
    n_lon,
    n_lat,
    depth_hbm,
    ground_hbm,
    rough_hbm,
    river_hbm,
    width_hbm,
    bank_hbm,
    mask_hbm,
    ext,
    sides,
    strips,
    own_mask,
    floats,
    ints,
    mask_in,
    top,
    bottom,
    load_sem,
    send_sem,
    recv_sem,
):
    lon = lax.axis_index("lon")
    lat = lax.axis_index("lat")
    east = lax.rem(lon + 1, n_lon)
    west = lax.rem(lon + n_lon - 1, n_lon)
    north = lax.rem(lat + 1, n_lat)
    south = lax.rem(lat + n_lat - 1, n_lat)
    around = [
        (east, lat),
        (west, lat),
        (lon, north),
        (lon, south),
        (east, north),
        (west, north),
        (east, south),
        (west, south),
    ]
    around = [{"lon": a, "lat": b} for a, b in around]
    barrier = pltpu.get_barrier_semaphore()
    for device in around:
        pl.semaphore_signal(barrier, inc=1, device_id=device, device_id_type=MESH)

    loads = []
    for number, (source, target) in enumerate(
        [
            (ground_hbm, floats.at[GROUND]),
            (bank_hbm, ints.at[0]),
            (width_hbm, ints.at[1]),
            (river_hbm, floats.at[RIVER]),
            (depth_hbm, floats.at[DEPTH]),
            (rough_hbm, floats.at[ROUGH]),
            (mask_hbm, mask_in),
        ]
    ):
        copy = pltpu.make_async_copy(source, target, load_sem.at[number])
        copy.start()
        loads.append(copy)

    def place(field, values):
        for tile in range(2):
            ext[field, tile, HALO : HALO + COLS, :] = values[tile * LANES : (tile + 1) * LANES, :].T
        top[field] = values[0:8, :]
        bottom[field] = values[ROWS - 8 : ROWS, :]

    loads[0].wait()
    ground = floats[GROUND]
    place(GROUND, ground)
    loads[1].wait()
    place(BED, ground - (1.0 + 0.5 * ints[0].astype(F32)))
    loads[2].wait()
    place(WIDTH, 8.0 + 9.0 * ints[1].astype(F32))
    loads[3].wait()
    place(RIVER, floats[RIVER])
    loads[4].wait()
    place(DEPTH, floats[DEPTH])
    loads[5].wait()
    place(ROUGH, floats[ROUGH])
    loads[6].wait()
    for tile in range(2):
        own_mask[tile] = jnp.broadcast_to(mask_in[tile : tile + 1, :].astype(F32), (8, LANES))
    top[6] = own_mask[0]
    bottom[6] = own_mask[1]

    pl.semaphore_wait(barrier, len(around))
    fields = pl.ds(0, 6)
    both = pl.ds(0, 2)
    sends = [
        (
            ext.at[fields, both, pl.ds(COLS, HALO), :],
            ext.at[fields, both, pl.ds(0, HALO), :],
            around[0],
        ),
        (
            ext.at[fields, both, pl.ds(HALO, HALO), :],
            ext.at[fields, both, pl.ds(HALO + COLS, HALO), :],
            around[1],
        ),
        (bottom, strips.at[FROM_SW], around[4]),
        (bottom, strips.at[FROM_SE], around[5]),
        (top, strips.at[FROM_NW], around[6]),
        (top, strips.at[FROM_NE], around[7]),
        (bottom, strips.at[FROM_S], around[2]),
        (top, strips.at[FROM_N], around[3]),
        (own_mask, sides.at[0], around[0]),
        (own_mask, sides.at[1], around[1]),
    ]
    copies = []
    for number, (source, target, device) in enumerate(sends):
        copy = pltpu.make_async_remote_copy(
            src_ref=source,
            dst_ref=target,
            send_sem=send_sem.at[number],
            recv_sem=recv_sem.at[number],
            device_id=device,
            device_id_type=MESH,
        )
        copy.start()
        copies.append(copy)
    for copy in copies:
        copy.wait()


def quotient(current, height, drop, friction, drive):
    power = jnp.exp2(POWER * jnp.log(height * height + SHALLOW * SHALLOW))
    resisted = 1.0 + friction * jnp.abs(current) * power
    return (current - drive * (height * drop)) / resisted


def flow_kernel(
    n_lat,
    ext,
    sides,
    strips,
    own_mask,
    flood_out,
    river_out,
    east_out,
    north_out,
    third,
    g,
    fl,
    sur,
    q_east,
    q_north,
    e_base,
    e_fric,
    n_base,
    n_fric,
    level,
    flux,
    bed,
    r_base,
    r_drive,
    r_fric,
    r_inv,
    give,
    total,
    spread,
):
    lat = lax.axis_index("lat")
    lane = lax.broadcasted_iota(jnp.int32, (8, LANES), 1)
    sublane = lax.broadcasted_iota(jnp.int32, (8, LANES), 0)
    last_lane = lane == LANES - 1
    first_lane = lane == 0

    ones = jnp.full((112, LANES), 1.0, F32)
    for field in range(6):
        for from_n, from_s, source, target, count in (
            (FROM_NW, FROM_SW, COLS - HALO, 0, HALO),
            (FROM_N, FROM_S, 0, HALO, COLS),
            (FROM_NE, FROM_SE, 0, HALO + COLS, HALO),
        ):
            block = jnp.concatenate([strips[from_n, field], ones, strips[from_s, field]], axis=0).T
            third[field, target : target + count, :] = block[source : source + count, :]

    def load(field, tile, j):
        if tile < 2:
            return ext[field, tile, pl.ds(j, 8, stride=SEG), :]
        return third[field, pl.ds(j, 8, stride=SEG), :]

    def after(values, j):
        return values[j + 1] if j + 1 < SEG else pltpu.roll(values[0], 7, 0)

    def before(values, j):
        return values[j - 1] if j else pltpu.roll(values[SEG - 1], 1, 0)

    def northward(values, tile):
        here = pltpu.roll(values[tile], LANES - 1, 1)
        there = pltpu.roll(values[(tile + 1) % TILES], LANES - 1, 1)
        return jnp.where(last_lane, there, here)

    def southward(values, tile):
        here = pltpu.roll(values[tile], 1, 1)
        there = pltpu.roll(values[(tile + TILES - 1) % TILES], 1, 1)
        return jnp.where(first_lane, there, here)

    near = lane < 64
    masks = []
    for tile in range(2):
        masks.append((sides[0, tile], own_mask[tile], sides[1, tile]))
    masks.append(
        tuple(
            jnp.where(near, strips[a, 6], strips[b, 6])
            for a, b in ((FROM_NW, FROM_SW), (FROM_N, FROM_S), (FROM_NE, FROM_SE))
        )
    )
    for tile in range(TILES):
        grounds = [load(GROUND, tile, j) for j in range(SEG)]
        roughs = [load(ROUGH, tile, j) for j in range(SEG)]
        for j in range(SEG):
            g[tile, j] = grounds[j]
            fl[tile, j] = load(DEPTH, tile, j)
            e_base[tile, j] = jnp.maximum(grounds[j], after(grounds, j))
            e_fric[tile, j] = (GRAVITY * TIME_STEP) * (roughs[j] * after(roughs, j))
            n_fric[tile, j] = roughs[j]
            q_east[tile, j] = jnp.zeros((8, LANES), F32)
            q_north[tile, j] = jnp.zeros((8, LANES), F32)
        beds = [load(BED, tile, j) for j in range(SEG)]
        widths = [load(WIDTH, tile, j) for j in range(SEG)]
        for j in range(SEG):
            column = sublane * SEG + j
            closed = (column == HALO - 1) | (column == HALO + COLS - 1) | (column == WIDE - 1)
            breadth = 0.5 * (widths[j] + after(widths, j))
            bed[tile, j] = beds[j]
            level[tile, j] = beds[j] + load(RIVER, tile, j)
            flux[tile, j] = jnp.zeros((8, LANES), F32)
            r_base[tile, j] = jnp.maximum(beds[j], after(beds, j))
            r_drive[tile, j] = jnp.where(
                closed, 0.0, (GRAVITY * SHORT_STEP / CELL_SIZE) * breadth
            )
            r_fric[tile, j] = (
                GRAVITY * SHORT_STEP * CHANNEL_MANNING * CHANNEL_MANNING
            ) / breadth
            r_inv[tile, j] = SHORT_STEP / (CELL_SIZE * widths[j])
            mask = jnp.where(
                column < HALO,
                masks[tile][0],
                jnp.where(column < HALO + COLS, masks[tile][1], masks[tile][2]),
            )
            give[tile, j] = mask * widths[j] * (SHORT_STEP * EXCHANGE / CELL_SIZE)
    for j in range(SEG):
        grounds = [g[tile, j] for tile in range(TILES)]
        roughs = [n_fric[tile, j] for tile in range(TILES)]
        for tile in range(TILES):
            n_base[tile, j] = jnp.maximum(grounds[tile], northward(grounds, tile))
            n_fric[tile, j] = (GRAVITY * TIME_STEP) * (roughs[tile] * northward(roughs, tile))

    drive = GRAVITY * TIME_STEP / CELL_SIZE
    n_drive = [
        jnp.full((8, LANES), drive, F32),
        jnp.where(last_lane & (lat == n_lat - 1), 0.0, drive),
        jnp.where(last_lane & (lat == 0), 0.0, drive),
    ]

    for step in range(STEPS):
        tiles = TILES if step < STEPS - 1 else 2
        for tile in range(TILES):
            for j in range(SEG):
                sur[tile, j] = g[tile, j] + fl[tile, j]
                total[tile, j] = jnp.zeros((8, LANES), F32)

        for tile in range(tiles):
            surfaces = [sur[tile, j] for j in range(SEG)]
            for j in range(SEG):
                east = after(surfaces, j)
                q_east[tile, j] = quotient(
                    q_east[tile, j],
                    jnp.maximum(surfaces[j], east) - e_base[tile, j],
                    east - surfaces[j],
                    e_fric[tile, j],
                    drive,
                )
        for j in range(SEG):
            surfaces = [sur[tile, j] for tile in range(TILES)]
            for tile in range(TILES):
                north = northward(surfaces, tile)
                q_north[tile, j] = quotient(
                    q_north[tile, j],
                    jnp.maximum(surfaces[tile], north) - n_base[tile, j],
                    north - surfaces[tile],
                    n_fric[tile, j],
                    n_drive[tile],
                )

        def substep(_, carry):
            for tile in range(tiles):
                first = level[tile, 0]
                first_flux = None
                here = first
                last_flux = None
                for j in range(SEG):
                    there = level[tile, j + 1] if j + 1 < SEG else pltpu.roll(first, 7, 0)
                    out = quotient(
                        flux[tile, j],
                        jnp.maximum(here, there) - r_base[tile, j],
                        there - here,
                        r_fric[tile, j],
                        r_drive[tile, j],
                    )
                    flux[tile, j] = out
                    total[tile, j] += here
                    if j:
                        level[tile, j] = (
                            here
                            - (SHORT_STEP * EXCHANGE) * (here - sur[tile, j])
                            + (last_flux - out) * r_inv[tile, j]
                        )
                    else:
                        first_flux = out
                    last_flux = out
                    here = there
                level[tile, 0] = (
                    first
                    - (SHORT_STEP * EXCHANGE) * (first - sur[tile, 0])
                    + (pltpu.roll(last_flux, 1, 0) - first_flux) * r_inv[tile, 0]
                )
            return carry

        lax.fori_loop(0, SUB, substep, 0)

        for j in range(SEG):
            norths = [q_north[tile, j] for tile in range(TILES)]
            for tile in range(tiles):
                east = q_east[tile, j]
                west = q_east[tile, j - 1] if j else pltpu.roll(q_east[tile, SEG - 1], 1, 0)
                flooded = fl[tile, j] + (TIME_STEP / CELL_SIZE) * (
                    west - east + southward(norths, tile) - norths[tile]
                )
                fl[tile, j] = flooded + give[tile, j] * (total[tile, j] - SUB * sur[tile, j])

    own = pl.ds(HALO, COLS)
    for number, (source, target) in enumerate(
        ((fl, flood_out), (level, river_out), (q_east, east_out), (q_north, north_out))
    ):
        for tile in range(2):
            for j in range(SEG):
                value = source[tile, j]
                if number == 1:
                    column = sublane * SEG + j
                    value = value - bed[tile, j]
                    before_all = load(RIVER, tile, j)
                    value = jnp.where(own_mask[tile] > 0.0, value, before_all)
                spread[tile, pl.ds(j, 8, stride=SEG), :] = value
            target[tile * LANES : (tile + 1) * LANES, :] = spread[tile, own, :].T


def body(n_lon, n_lat, depth_init, ground, roughness, river_init, reach_mask, width_class, bank_class):
    mask = reach_mask.reshape(2, LANES)
    field = (ROWS, COLS)
    anywhere = pl.BlockSpec(memory_space=pl.ANY)
    near = pl.BlockSpec(memory_space=pltpu.VMEM)
    ext, sides, strips, own_mask = pl.pallas_call(
        functools.partial(exchange_kernel, n_lon, n_lat),
        out_shape=(
            jax.ShapeDtypeStruct((6, 2, WIDE, LANES), F32),
            jax.ShapeDtypeStruct((2, 2, 8, LANES), F32),
            jax.ShapeDtypeStruct((6, 7, 8, LANES), F32),
            jax.ShapeDtypeStruct((2, 8, LANES), F32),
        ),
        in_specs=[anywhere] * 7,
        out_specs=(near,) * 4,
        scratch_shapes=[
            pltpu.VMEM((4, ROWS, COLS), F32),
            pltpu.VMEM((2, ROWS, COLS), jnp.int32),
            pltpu.VMEM((2, LANES), jnp.int32),
            pltpu.VMEM((7, 8, LANES), F32),
            pltpu.VMEM((7, 8, LANES), F32),
            pltpu.SemaphoreType.DMA((7,)),
            pltpu.SemaphoreType.DMA((10,)),
            pltpu.SemaphoreType.DMA((10,)),
        ],
        compiler_params=pltpu.CompilerParams(collective_id=0, has_side_effects=True),
        name="exchange",
    )(depth_init, ground, roughness, river_init, width_class, bank_class, mask)
    state = pltpu.VMEM((TILES, SEG, 8, LANES), F32)
    return pl.pallas_call(
        functools.partial(flow_kernel, n_lat),
        out_shape=(jax.ShapeDtypeStruct(field, F32),) * 4,
        in_specs=[near] * 4,
        out_specs=(near,) * 4,
        scratch_shapes=[pltpu.VMEM((6, WIDE, LANES), F32)]
        + [state] * 18
        + [pltpu.VMEM((2, WIDE, LANES), F32)],
        name="flow",
    )(ext, sides, strips, own_mask)


def solution(mesh):
    placed = P("lat", "lon")
    return jax.shard_map(
        functools.partial(body, mesh.shape["lon"], mesh.shape["lat"]),
        mesh=mesh,
        in_specs=(placed,) * 7,
        out_specs=(placed,) * 4,
        check_vma=False,
    )
```

time: 135 us -> 41.9 us (0.31)
  the two profiles are of different devices: /device:TPU:134 before, /device:TPU:14 now
where the time goes in v1:
time: 41.9 us; the launch traced here: 41.7 us
  Pallas kernels  41.1 us (98%)
  between operations  0.64 us (2%)
    pallas_call x1, Pallas kernels, body(): pl.pallas_call(functools.partial(exchange_kernel, n_lon, n_lat), out_shap...  29.4 us
    pallas_call x1, Pallas kernels, body(): pl.pallas_call(functools.partial(flow_kernel, n_lat), out_shape=(jax.Shap...  11.7 us

profile of v1, /device:TPU:14, one launch (start us, length us, event | category | flops | bytes accessed | tf_op | source)
XLA Modules:
  0.0 41.7 jit_solution(8728006245489444999)
XLA Ops:
  0.6 29.4 %exchange.1 = (f32[6,2,176,128]{3,2,1,0:T(8,128)}, f32[2,2,8,128]{3,2,1,0:T(8,128)}, f32[6,7,8,128]{3,2,1,0:T(8,128)}, f32[2,8,128]{2,1,0:T(8,128)}) custom-call(f32[256,128]{1,0:T(8,128)} %depth_hbm.1, f32[256,128]{1,0:T(8,128)} %ground_hbm.1, f32[256,128]{1,0:T(8,128)} %rough_hbm.1, f32[256,128]{1,0:T(8,128)} %river_hbm.1, s32[256,128]{1,0:T(8,128)} %width_hbm.1, ...), custom_call_target="tpu_custom_call" | custom-call | tf_op jit(solution)/shard_map/exchange/pallas_call | solution.py:388
  30.0 11.7 %flow.1 = (f32[256,128]{1,0:T(8,128)}, f32[256,128]{1,0:T(8,128)}, f32[256,128]{1,0:T(8,128)}, f32[256,128]{1,0:T(8,128)}) custom-call(f32[6,2,176,128]{3,2,1,0:T(8,128)} %get-tuple-element.8.ext, f32[2,2,8,128]{3,2,1,0:T(8,128)} %get-tuple-element.9.sides, f32[6,7,8,128]{3,2,1,0:T(8,128)} %get-tuple-element.10.strips, f32[2,8,128]{2,1,0:T(8,128)} %get-tuple-element.11.own_mask), custom_call_target="tpu_custom_call" | custom-call | tf_op jit(solution)/shard_map/flow/pallas_call | solution.py:412

commit v2 on v1

v2 whole, which is shorter than its diff:
```python
import functools
import math

import jax
import jax.numpy as jnp
from jax import lax
from jax.experimental import pallas as pl
from jax.experimental.pallas import tpu as pltpu
from jax.sharding import PartitionSpec as P

MESH = pl.DeviceIdType.MESH
F32 = jnp.float32
SUB = 8
STEPS = 4
ROWS = 256
COLS = 128
HALO = 24
WIDE = COLS + 2 * HALO
LANES = 128
STRIP = 40
BAND = 96
STARTS = (0, 8, 16, 16)
DEPTH, GROUND, ROUGH, RIVER, WIDTH, BED = range(6)
FROM_S, FROM_N, FROM_SW, FROM_SE, FROM_NW, FROM_NE = range(6)
FLOOD, LEVEL, EAST, NORTH, FLUX = range(5)

GRAVITY = 9.81
CELL_SIZE = 90.0
TIME_STEP = 10.0
SHALLOW = 0.1
EXCHANGE = 0.01
CHANNEL_MANNING = 0.035
SHORT_STEP = TIME_STEP / SUB
POWER = -7.0 / 6.0 / math.log(2.0)
DRIVE = GRAVITY * TIME_STEP / CELL_SIZE

STATE = 5
SCRATCH = 17
REGISTERS = 32
VMEM_LIMIT = 24 << 20


def quotient(current, height, drop, friction, drive):
    power = jnp.exp2(POWER * jnp.log(height * height + SHALLOW * SHALLOW))
    resisted = 1.0 + friction * jnp.abs(current) * power
    return (current - drive * (height * drop)) / resisted


class Zone:
    def __init__(self, refs, sizes, partners):
        self.sizes = sizes
        self.partners = partners
        self.base = [sum(sizes[:t]) for t in range(len(sizes))]
        self.state = refs[:STATE]
        (
            self.g,
            self.sur,
            self.e_base,
            self.e_fric,
            self.n_base,
            self.n_fric,
            self.r_base,
            self.r_drive,
            self.r_fric,
            self.r_inv,
            self.give,
            self.total,
        ) = refs[STATE:]
        self.lane = lax.broadcasted_iota(jnp.int32, (8, LANES), 1)
        self.sublane = lax.broadcasted_iota(jnp.int32, (8, LANES), 0)

    def column(self, tile, j):
        return self.sublane * self.sizes[tile] + j

    def northward(self, read, tile):
        here = pltpu.roll(read(tile), LANES - 1, 1)
        if self.partners[tile] == tile:
            return here
        there = pltpu.roll(read(self.partners[tile]), LANES - 1, 1)
        return jnp.where(self.lane == LANES - 1, there, here)

    def southward(self, read, tile):
        here = pltpu.roll(read(tile), 1, 1)
        if self.partners[tile] == tile:
            return here
        there = pltpu.roll(read(self.partners[tile]), 1, 1)
        return jnp.where(self.lane == 0, there, here)

    def prepare(self, tile, load, closed, mask):
        size, base = self.sizes[tile], self.base[tile]

        def after(values, j):
            return values[j + 1] if j + 1 < size else pltpu.roll(values[0], 7, 0)

        grounds = [load(GROUND, j) for j in range(size)]
        roughs = [load(ROUGH, j) for j in range(size)]
        beds = [load(BED, j) for j in range(size)]
        widths = [load(WIDTH, j) for j in range(size)]
        for j in range(size):
            at = base + j
            column = self.column(tile, j)
            self.g[at] = grounds[j]
            self.e_base[at] = jnp.maximum(grounds[j], after(grounds, j))
            self.e_fric[at] = (GRAVITY * TIME_STEP) * (roughs[j] * after(roughs, j))
            self.n_fric[at] = roughs[j]
            breadth = 0.5 * (widths[j] + after(widths, j))
            self.r_base[at] = jnp.maximum(beds[j], after(beds, j))
            self.r_drive[at] = jnp.where(
                closed(column), 0.0, (GRAVITY * SHORT_STEP / CELL_SIZE) * breadth
            )
            self.r_fric[at] = (
                GRAVITY * SHORT_STEP * CHANNEL_MANNING * CHANNEL_MANNING
            ) / breadth
            self.r_inv[at] = SHORT_STEP / (CELL_SIZE * widths[j])
            self.give[at] = mask(column) * widths[j] * (SHORT_STEP * EXCHANGE / CELL_SIZE)

    def prepare_north(self, tiles):
        for j in range(self.sizes[tiles[0]]):
            grounds = {t: self.g[self.base[t] + j] for t in tiles}
            roughs = {t: self.n_fric[self.base[t] + j] for t in tiles}
            for t in tiles:
                at = self.base[t] + j
                self.n_base[at] = jnp.maximum(grounds[t], self.northward(grounds.get, t))
                self.n_fric[at] = (GRAVITY * TIME_STEP) * (
                    roughs[t] * self.northward(roughs.get, t)
                )

    def begin(self, tile, load):
        for j in range(self.sizes[tile]):
            at = self.base[tile] + j
            self.state[FLOOD][at] = load(DEPTH, j)
            self.state[LEVEL][at] = load(BED, j) + load(RIVER, j)
            for k in (EAST, NORTH, FLUX):
                self.state[k][at] = jnp.zeros((8, LANES), F32)

    def flows(self, pairs, drives):
        flood, _, q_east, q_north, _ = self.state
        for tiles in pairs:
            for t in tiles:
                for j in range(self.sizes[t]):
                    at = self.base[t] + j
                    self.sur[at] = self.g[at] + flood[at]
                    self.total[at] = jnp.zeros((8, LANES), F32)
        for tiles in pairs:
            for t in tiles:
                base, size = self.base[t], self.sizes[t]
                for j in range(size):
                    here = self.sur[base + j]
                    there = (
                        self.sur[base + j + 1] if j + 1 < size else pltpu.roll(self.sur[base], 7, 0)
                    )
                    q_east[base + j] = quotient(
                        q_east[base + j],
                        jnp.maximum(here, there) - self.e_base[base + j],
                        there - here,
                        self.e_fric[base + j],
                        DRIVE,
                    )
        for tiles in pairs:
            for j in range(self.sizes[tiles[0]]):
                surfaces = {t: self.sur[self.base[t] + j] for t in tiles}
                for t in tiles:
                    at = self.base[t] + j
                    there = self.northward(surfaces.get, t)
                    q_north[at] = quotient(
                        q_north[at],
                        jnp.maximum(surfaces[t], there) - self.n_base[at],
                        there - surfaces[t],
                        self.n_fric[at],
                        drives[t],
                    )

    def rivers(self):
        level, flux = self.state[LEVEL], self.state[FLUX]
        rate = SHORT_STEP * EXCHANGE

        def substep(_, carry):
            for t, size in enumerate(self.sizes):
                base = self.base[t]
                first = level[base]
                here = first
                first_flux = None
                last_flux = None
                for j in range(size):
                    at = base + j
                    there = level[at + 1] if j + 1 < size else pltpu.roll(first, 7, 0)
                    out = quotient(
                        flux[at],
                        jnp.maximum(here, there) - self.r_base[at],
                        there - here,
                        self.r_fric[at],
                        self.r_drive[at],
                    )
                    flux[at] = out
                    self.total[at] += here
                    if j:
                        level[at] = (
                            here
                            - rate * (here - self.sur[at])
                            + (last_flux - out) * self.r_inv[at]
                        )
                    else:
                        first_flux = out
                    last_flux = out
                    here = there
                level[base] = (
                    first
                    - rate * (first - self.sur[base])
                    + (pltpu.roll(last_flux, 1, 0) - first_flux) * self.r_inv[base]
                )
            return carry

        lax.fori_loop(0, SUB, substep, 0)

    def floods(self, pairs):
        flood, _, q_east, q_north, _ = self.state
        for tiles in pairs:
            for j in range(self.sizes[tiles[0]]):
                norths = {t: q_north[self.base[t] + j] for t in tiles}
                for t in tiles:
                    base, size = self.base[t], self.sizes[t]
                    at = base + j
                    west = q_east[at - 1] if j else pltpu.roll(q_east[base + size - 1], 1, 0)
                    flooded = flood[at] + (TIME_STEP / CELL_SIZE) * (
                        west - q_east[at] + self.southward(norths.get, t) - norths[t]
                    )
                    flood[at] = flooded + self.give[at] * (self.total[at] - SUB * self.sur[at])


def fold(low, high):
    lane = lax.broadcasted_iota(jnp.int32, (8, LANES), 1)
    return jnp.where(lane < 64, pltpu.roll(low, 16, 1), high)


def exchange_kernel(
    n_lon,
    n_lat,
    depth_hbm,
    ground_hbm,
    rough_hbm,
    river_hbm,
    width_hbm,
    bank_hbm,
    mask_hbm,
    ext,
    sides,
    strips,
    own_mask,
    inner,
    band,
    floats,
    ints,
    mask_in,
    top,
    bottom,
    load_sem,
    send_sem,
    recv_sem,
    *scratch,
):
    lon = lax.axis_index("lon")
    lat = lax.axis_index("lat")
    east = lax.rem(lon + 1, n_lon)
    west = lax.rem(lon + n_lon - 1, n_lon)
    north = lax.rem(lat + 1, n_lat)
    south = lax.rem(lat + n_lat - 1, n_lat)
    around = [
        (east, lat),
        (west, lat),
        (lon, north),
        (lon, south),
        (east, north),
        (west, north),
        (east, south),
        (west, south),
    ]
    around = [{"lon": a, "lat": b} for a, b in around]
    barrier = pltpu.get_barrier_semaphore()
    for device in around:
        pl.semaphore_signal(barrier, inc=1, device_id=device, device_id_type=MESH)

    loads = []
    for number, (source, target) in enumerate(
        [
            (ground_hbm, floats.at[GROUND]),
            (bank_hbm, ints.at[0]),
            (width_hbm, ints.at[1]),
            (river_hbm, floats.at[RIVER]),
            (depth_hbm, floats.at[DEPTH]),
            (rough_hbm, floats.at[ROUGH]),
            (mask_hbm, mask_in),
        ]
    ):
        copy = pltpu.make_async_copy(source, target, load_sem.at[number])
        copy.start()
        loads.append(copy)

    def place(field, values):
        for tile in range(2):
            ext[field, tile, HALO : HALO + COLS, :] = values[tile * LANES : (tile + 1) * LANES, :].T
        top[field] = values[0:8, :]
        bottom[field] = values[ROWS - 8 : ROWS, :]

    loads[0].wait()
    ground = floats[GROUND]
    place(GROUND, ground)
    loads[1].wait()
    place(BED, ground - (1.0 + 0.5 * ints[0].astype(F32)))
    loads[2].wait()
    place(WIDTH, 8.0 + 9.0 * ints[1].astype(F32))
    loads[3].wait()
    place(RIVER, floats[RIVER])
    loads[4].wait()
    place(DEPTH, floats[DEPTH])
    loads[5].wait()
    place(ROUGH, floats[ROUGH])
    loads[6].wait()
    for tile in range(2):
        own_mask[tile] = jnp.broadcast_to(mask_in[tile : tile + 1, :].astype(F32), (8, LANES))
    top[6] = own_mask[0]
    bottom[6] = own_mask[1]

    pl.semaphore_wait(barrier, len(around))
    fields = pl.ds(0, 6)
    both = pl.ds(0, 2)
    sends = [
        (
            ext.at[fields, both, pl.ds(COLS, HALO), :],
            ext.at[fields, both, pl.ds(0, HALO), :],
            around[0],
        ),
        (
            ext.at[fields, both, pl.ds(HALO, HALO), :],
            ext.at[fields, both, pl.ds(HALO + COLS, HALO), :],
            around[1],
        ),
        (bottom, strips.at[FROM_SW], around[4]),
        (bottom, strips.at[FROM_SE], around[5]),
        (top, strips.at[FROM_NW], around[6]),
        (top, strips.at[FROM_NE], around[7]),
        (bottom, strips.at[FROM_S], around[2]),
        (top, strips.at[FROM_N], around[3]),
        (own_mask, sides.at[0], around[0]),
        (own_mask, sides.at[1], around[1]),
    ]
    copies = []
    for number, (source, target, device) in enumerate(sends):
        copy = pltpu.make_async_remote_copy(
            src_ref=source,
            dst_ref=target,
            send_sem=send_sem.at[number],
            recv_sem=recv_sem.at[number],
            device_id=device,
            device_id_type=MESH,
        )
        copy.start()
        copies.append(copy)

    size = COLS // 8
    zone = Zone(scratch, [size, size], [1, 0])
    for tile in range(2):
        def load(field, j):
            return ext[field, tile, pl.ds(HALO + j, 8, stride=size), :]

        zone.prepare(tile, load, lambda c: c == COLS - 1, lambda c: own_mask[tile])
        zone.begin(tile, load)
    pairs = [(0, 1)]
    zone.prepare_north((0, 1))
    drives = [DRIVE, jnp.where((zone.lane == LANES - 1) & (lat == n_lat - 1), 0.0, DRIVE)]

    def step(number, carry):
        zone.flows(pairs, drives)
        zone.rivers()
        zone.floods(pairs)
        for k in range(STATE):
            for tile in range(2):
                for j in range(size):
                    inner[number, k, tile, pl.ds(j, 8, stride=size), :] = zone.state[k][
                        zone.base[tile] + j
                    ]
        return carry

    lax.fori_loop(0, STEPS, step, 0)

    for field in range(6):
        values = [
            fold(
                ext[field, 0, HALO + 8 * i : HALO + 8 * i + 8, :],
                ext[field, 1, HALO + 8 * i : HALO + 8 * i + 8, :],
            )
            for i in range(size)
        ]
        for i in range(BAND // 8):
            value = jnp.ones((8, LANES), F32)
            for k in range(4):
                at = 4 * k - 4 + i
                if 0 <= at < size:
                    moved = pltpu.roll(values[at], (32 * k + 8) % LANES, 1)
                    value = jnp.where(zone.lane // 32 == k, moved, value)
            band[field, 8 * i : 8 * i + 8, :] = value

    for copy in copies:
        copy.wait()


def flow_kernel(
    n_lat,
    ext,
    sides,
    strips,
    own_mask,
    inner,
    band,
    flood_out,
    river_out,
    east_out,
    north_out,
    rows,
    plain,
    ends,
    *scratch,
):
    lat = lax.axis_index("lat")
    size = STRIP // 8
    wide = BAND // 8
    zone = Zone(scratch, [size] * 4 + [wide], [1, 0, 3, 2, 4])
    lane, sublane = zone.lane, zone.sublane
    group, place = lane // 32, lane % 32
    halo_lane = (place >= 8) & (place < 24)
    row_tile = 4
    pairs = [(0, 1), (2, 3), (4,)]
    last_row = (lane == LANES - 1) & (lat == n_lat - 1)
    plain_drive = jnp.where(last_row, 0.0, DRIVE)
    row_closed = ((place == 7) & (lat == n_lat - 1)) | ((place == 23) & (lat == 0))
    drives = [DRIVE, plain_drive, DRIVE, plain_drive, jnp.where(row_closed, 0.0, DRIVE)]

    ones = jnp.ones((8, LANES), F32)
    for field in range(6):
        pieces = []
        for k in range(4):
            pieces.append(ones)
            for west, middle, east in (
                (FROM_NW, FROM_N, FROM_NE),
                (FROM_SW, FROM_S, FROM_SE),
            ):
                value = strips[middle, field]
                if k != 1:
                    value = pltpu.roll(value, (160 - 32 * k) % LANES, 1)
                if k == 0:
                    value = jnp.where(lane < 32, pltpu.roll(strips[west, field], 32, 1), value)
                if k == 3:
                    value = jnp.where(lane < 64, value, pltpu.roll(strips[east, field], 64, 1))
                pieces.append(value)
            pieces.append(ones)
        block = jnp.concatenate(pieces, axis=0).T
        for i in range(wide):
            value = band[field, 8 * i : 8 * i + 8, :]
            if 1 <= i < 4:
                at = 8 * (i - 1)
                moved = fold(ext[field, 0, at : at + 8, :], ext[field, 1, at : at + 8, :])
                value = jnp.where(group == 0, pltpu.roll(moved, 8, 1), value)
            if 8 <= i < 11:
                at = HALO + COLS + 8 * (i - 8)
                moved = fold(ext[field, 0, at : at + 8, :], ext[field, 1, at : at + 8, :])
                value = jnp.where(group == 3, pltpu.roll(moved, 104, 1), value)
            rows[field, 8 * i : 8 * i + 8, :] = jnp.where(
                halo_lane, block[8 * i : 8 * i + 8, :], value
            )

    def row_mask(low, high, north, south):
        value = jnp.where(place < 8, pltpu.roll(high, 8, 1), pltpu.roll(low, 24, 1))
        value = jnp.where(halo_lane & (place < 16), pltpu.roll(north, 8, 1), value)
        return jnp.where(halo_lane & (place >= 16), pltpu.roll(south, 24, 1), value)

    middle = row_mask(own_mask[0], own_mask[1], strips[FROM_N, 6], strips[FROM_S, 6])
    west = row_mask(sides[0, 0], sides[0, 1], strips[FROM_NW, 6], strips[FROM_SW, 6])
    east = row_mask(sides[1, 0], sides[1, 1], strips[FROM_NE, 6], strips[FROM_SE, 6])
    east = pltpu.roll(east, 96, 1)
    spread = middle
    for k in range(1, 4):
        spread = jnp.where(group == k, pltpu.roll(middle, 32 * k, 1), spread)

    def load_row(field, j):
        return rows[field, pl.ds(j, 8, stride=wide), :]

    zone.prepare(
        row_tile,
        load_row,
        lambda c: ((c == 31) & (group == 0)) | ((c == 63) & (group == 3)) | (c == BAND - 1),
        lambda c: jnp.where(
            (c < 32) & (group == 0), west, jnp.where((c >= 64) & (group == 3), east, spread)
        ),
    )
    zone.begin(row_tile, load_row)
    zone.prepare_north((row_tile,))

    def start_of(step, side):
        return STARTS[step] if side == 0 else WIDE - STRIP - STARTS[step]

    for step in range(STEPS):
        for side in range(2):
            start = start_of(step, side)
            for tile in range(2):
                t = 2 * side + tile

                def load(field, j):
                    return ext[field, tile, pl.ds(start + j, 8, stride=size), :]

                if step != 3:
                    zone.prepare(
                        t,
                        load,
                        lambda c: (c + start == HALO - 1)
                        | (c + start == HALO + COLS - 1)
                        | (c == STRIP - 1),
                        lambda c: jnp.where(
                            (c + start < HALO) if side == 0 else (c + start >= HALO + COLS),
                            sides[side, tile],
                            own_mask[tile],
                        ),
                    )
                if step == 0:
                    zone.begin(t, load)
                else:
                    for k in range(STATE):
                        if side == 0:
                            low, high = 8 * step, start + STRIP - HALO
                        else:
                            low, high = start - HALO, COLS - 8 * step
                        plain[k, tile, HALO + low : HALO + high, :] = inner[
                            step - 1, k, tile, low:high, :
                        ]
                        for j in range(size):
                            zone.state[k][zone.base[t] + j] = plain[
                                k, tile, pl.ds(start + j, 8, stride=size), :
                            ]
            if step != 3:
                zone.prepare_north((2 * side, 2 * side + 1))
        zone.flows(pairs, drives)
        zone.rivers()
        zone.floods(pairs)
        for side in range(2):
            start = start_of(step, side)
            for tile in range(2):
                t = 2 * side + tile
                for k in range(STATE):
                    for j in range(size):
                        plain[k, tile, pl.ds(start + j, 8, stride=size), :] = zone.state[k][
                            zone.base[t] + j
                        ]

    for k in range(4):
        for j in range(wide):
            ends[k, pl.ds(j, 8, stride=wide), :] = zone.state[k][zone.base[row_tile] + j]
    for k, target in enumerate((flood_out, river_out, east_out, north_out)):
        for tile in range(2):
            pieces = []
            for i in range(COLS // 8):
                if 3 <= i < 13:
                    value = inner[STEPS - 1, k, tile, 8 * i : 8 * i + 8, :]
                else:
                    value = plain[k, tile, HALO + 8 * i : HALO + 8 * i + 8, :]
                end = ends[k, 32 + 8 * (i % 4) : 40 + 8 * (i % 4), :]
                shift = 32 * (i // 4)
                if tile == 0:
                    value = jnp.where(lane < 4, pltpu.roll(end, (104 - shift) % LANES, 1), value)
                else:
                    value = jnp.where(lane < 124, value, pltpu.roll(end, (120 - shift) % LANES, 1))
                if k == LEVEL:
                    at = HALO + 8 * i
                    value = jnp.where(
                        own_mask[tile] > 0.0,
                        value - ext[BED, tile, at : at + 8, :],
                        ext[RIVER, tile, at : at + 8, :],
                    )
                pieces.append(value)
            target[tile * LANES : (tile + 1) * LANES, :] = jnp.concatenate(pieces, axis=0).T


def body(n_lon, n_lat, depth_init, ground, roughness, river_init, reach_mask, width_class, bank_class):
    mask = reach_mask.reshape(2, LANES)
    field = (ROWS, COLS)
    far = pl.BlockSpec(memory_space=pltpu.HBM)
    near = pl.BlockSpec(memory_space=pltpu.VMEM)
    state = [pltpu.VMEM((REGISTERS, 8, LANES), F32)] * SCRATCH
    handed = pl.pallas_call(
        functools.partial(exchange_kernel, n_lon, n_lat),
        out_shape=(
            pltpu.VMEM((6, 2, WIDE, LANES), F32),
            pltpu.VMEM((2, 2, 8, LANES), F32),
            pltpu.VMEM((6, 7, 8, LANES), F32),
            pltpu.VMEM((2, 8, LANES), F32),
            pltpu.VMEM((STEPS, STATE, 2, COLS, LANES), F32),
            pltpu.VMEM((6, BAND, LANES), F32),
        ),
        in_specs=[far] * 7,
        out_specs=(near,) * 6,
        scratch_shapes=[
            pltpu.VMEM((4, ROWS, COLS), F32),
            pltpu.VMEM((2, ROWS, COLS), jnp.int32),
            pltpu.VMEM((2, LANES), jnp.int32),
            pltpu.VMEM((7, 8, LANES), F32),
            pltpu.VMEM((7, 8, LANES), F32),
            pltpu.SemaphoreType.DMA((7,)),
            pltpu.SemaphoreType.DMA((10,)),
            pltpu.SemaphoreType.DMA((10,)),
        ]
        + state,
        compiler_params=pltpu.CompilerParams(
            collective_id=0, has_side_effects=True, vmem_limit_bytes=VMEM_LIMIT
        ),
        name="exchange",
    )(*[
        pltpu.with_memory_space_constraint(x, pltpu.HBM)
        for x in (depth_init, ground, roughness, river_init, width_class, bank_class, mask)
    ])
    handed = [pltpu.with_memory_space_constraint(x, pltpu.VMEM) for x in handed]
    return pl.pallas_call(
        functools.partial(flow_kernel, n_lat),
        out_shape=(jax.ShapeDtypeStruct(field, F32),) * 4,
        in_specs=[near] * 6,
        out_specs=(near,) * 4,
        scratch_shapes=[
            pltpu.VMEM((6, BAND, LANES), F32),
            pltpu.VMEM((STATE, 2, WIDE, LANES), F32),
            pltpu.VMEM((4, BAND, LANES), F32),
        ]
        + state,
        compiler_params=pltpu.CompilerParams(vmem_limit_bytes=VMEM_LIMIT),
        name="flow",
    )(*handed)


def solution(mesh):
    placed = P("lat", "lon")
    return jax.shard_map(
        functools.partial(body, mesh.shape["lon"], mesh.shape["lat"]),
        mesh=mesh,
        in_specs=(placed,) * 7,
        out_specs=(placed,) * 4,
        check_vma=False,
    )
```

time: 41.9 us -> 36.7 us (0.88)
  Pallas kernels: 41.1 us -> 35.9 us
    pallas_call x1, Pallas kernels: 11.7 us -> 7.55 us  [body(): pl.pallas_call(functools.partial(flow_kernel, n_lat), out_shape=(jax.Shap...]
    pallas_call x1, Pallas kernels: 29.4 us -> 28.3 us  [body(): pl.pallas_call(functools.partial(exchange_kernel, n_lon, n_lat), out_shap...]
where the time goes in v2:
time: 36.7 us; the launch traced here: 36.5 us
  Pallas kernels  35.9 us (98%)
  between operations  0.64 us (2%)
    pallas_call x1, Pallas kernels, body(): pl.pallas_call(functools.partial(exchange_kernel, n_lon, n_lat), out_shap...  28.3 us
    pallas_call x1, Pallas kernels, body(): pl.pallas_call(functools.partial(flow_kernel, n_lat), out_shape=(jax.Shap...  7.55 us

profile of v2, /device:TPU:14, one launch (start us, length us, event | category | flops | bytes accessed | tf_op | source)
XLA Modules:
  0.0 36.5 jit_solution(9934803196837236991)
XLA Ops:
  0.6 28.3 %exchange.1 = (f32[6,2,176,128]{3,2,1,0:T(8,128)S(1)}, f32[2,2,8,128]{3,2,1,0:T(8,128)S(1)}, f32[6,7,8,128]{3,2,1,0:T(8,128)S(1)}, f32[2,8,128]{2,1,0:T(8,128)S(...) custom-call(f32[256,128]{1,0:T(8,128)} %depth_hbm.1, f32[256,128]{1,0:T(8,128)} %ground_hbm.1, ...), custom_call_target="tpu_custom_call" | custom-call | tf_op jit(solution)/shard_map/exchange/pallas_call | solution.py:586
  29.0 7.6 %flow.1 = (f32[256,128]{1,0:T(8,128)}, f32[256,128]{1,0:T(8,128)}, f32[256,128]{1,0:T(8,128)}, f32[256,128]{1,0:T(8,128)}) custom-call(f32[6,2,176,128]{3,2,1,0:T(8,128)S(1)} %get-tuple-element.10.ext, f32[2,2,8,128]{3,2,1,0:T(8,128)S(1)} %get-tuple-element.11.sides, f32[6,7,8,128]{3,2,1,0:T(8,128)S(1)} %get-tuple-element.12.strips, ...), custom_call_target="tpu_custom_call" | custom-call | tf_op jit(solution)/shard_map/flow/pallas_call | solution.py:618

commit v3 on v2

--- a/solution.py
+++ b/solution.py
@@ -17,7 +17,7 @@
 HALO = 24
 WIDE = COLS + 2 * HALO
 LANES = 128
-STRIP = 40
+STRIPS = (32, 32, 32, 40)
 BAND = 96
 STARTS = (0, 8, 16, 16)
 DEPTH, GROUND, ROUGH, RIVER, WIDTH, BED = range(6)
@@ -248,6 +248,7 @@
     own_mask,
     inner,
     band,
+    plain,
     floats,
     ints,
     mask_in,
@@ -399,8 +400,74 @@
                     value = jnp.where(zone.lane // 32 == k, moved, value)
             band[field, 8 * i : 8 * i + 8, :] = value
 
-    for copy in copies:
-        copy.wait()
+    side_copies = (0, 1, 8, 9)
+    for number in side_copies:
+        copies[number].wait()
+    for step in range(STEPS):
+        strip = STRIPS[step]
+        size = strip // 8
+        zone = Zone(scratch, [size] * 4, [1, 0, 3, 2])
+        pairs = [(0, 1), (2, 3)]
+        for side in range(2):
+            start = start_of(step, side)
+            for tile in range(2):
+                t = 2 * side + tile
+
+                def load(field, j):
+                    return ext[field, tile, pl.ds(start + j, 8, stride=size), :]
+
+                zone.prepare(
+                    t,
+                    load,
+                    lambda c: (c + start == HALO - 1)
+                    | (c + start == HALO + COLS - 1)
+                    | (c == strip - 1),
+                    lambda c: jnp.where(
+                        (c + start < HALO) if side == 0 else (c + start >= HALO + COLS),
+                        sides[side, tile],
+                        own_mask[tile],
+                    ),
+                )
+                if step == 0:
+                    zone.begin(t, load)
+                    continue
+                for k in range(STATE):
+                    if side == 0:
+                        low, high = 8 * (step - 1), start + strip - HALO
+                        edge, kept = low, zone.sublane == 0
+                    else:
+                        low, high = start - HALO, COLS - 8 * (step - 1)
+                        edge, kept = high - 8, zone.sublane == 7
+                    for at in range(low, high, 8):
+                        value = inner[step - 1, k, tile, at : at + 8, :]
+                        if step == 1 and at == edge and k in (FLOOD, EAST):
+                            old = plain[k, tile, HALO + at : HALO + at + 8, :]
+                            value = jnp.where(kept, old, value)
+                        plain[k, tile, HALO + at : HALO + at + 8, :] = value
+                    for j in range(size):
+                        zone.state[k][zone.base[t] + j] = plain[
+                            k, tile, pl.ds(start + j, 8, stride=size), :
+                        ]
+            zone.prepare_north((2 * side, 2 * side + 1))
+        zone.flows(pairs, [drives[0], drives[1], drives[0], drives[1]])
+        zone.rivers()
+        zone.floods(pairs)
+        for side in range(2):
+            start = start_of(step, side)
+            for tile in range(2):
+                t = 2 * side + tile
+                for k in range(STATE if step < STEPS - 1 else 4):
+                    for j in range(size):
+                        plain[k, tile, pl.ds(start + j, 8, stride=size), :] = zone.state[k][
+                            zone.base[t] + j
+                        ]
+    for number, copy in enumerate(copies):
+        if number not in side_copies:
+            copy.wait()
+
+
+def start_of(step, side):
+    return STARTS[step] if side == 0 else WIDE - STRIPS[step] - STARTS[step]
 
 
 def flow_kernel(
@@ -411,28 +478,50 @@
     own_mask,
     inner,
     band,
+    plain,
     flood_out,
     river_out,
     east_out,
     north_out,
     rows,
-    plain,
     ends,
+    stage,
+    sems,
     *scratch,
 ):
     lat = lax.axis_index("lat")
-    size = STRIP // 8
     wide = BAND // 8
-    zone = Zone(scratch, [size] * 4 + [wide], [1, 0, 3, 2, 4])
+    zone = Zone(scratch, [wide], [0])
     lane, sublane = zone.lane, zone.sublane
     group, place = lane // 32, lane % 32
     halo_lane = (place >= 8) & (place < 24)
-    row_tile = 4
-    pairs = [(0, 1), (2, 3), (4,)]
-    last_row = (lane == LANES - 1) & (lat == n_lat - 1)
-    plain_drive = jnp.where(last_row, 0.0, DRIVE)
+    pairs = [(0,)]
     row_closed = ((place == 7) & (lat == n_lat - 1)) | ((place == 23) & (lat == 0))
-    drives = [DRIVE, plain_drive, DRIVE, plain_drive, jnp.where(row_closed, 0.0, DRIVE)]
+    drives = [jnp.where(row_closed, 0.0, DRIVE)]
+    outs = (flood_out, river_out, east_out, north_out)
+
+    copies = []
+    for k in (EAST, NORTH, FLOOD, LEVEL):
+        for tile in range(2):
+            pieces = []
+            for i in range(COLS // 8):
+                if 3 <= i < 13:
+                    value = inner[STEPS - 1, k, tile, 8 * i : 8 * i + 8, :]
+                else:
+                    value = plain[k, tile, HALO + 8 * i : HALO + 8 * i + 8, :]
+                if k == LEVEL:
+                    at = HALO + 8 * i
+                    value = jnp.where(
+                        own_mask[tile] > 0.0,
+                        value - ext[BED, tile, at : at + 8, :],
+                        ext[RIVER, tile, at : at + 8, :],
+                    )
+                pieces.append(value)
+            stage[k, tile * LANES : (tile + 1) * LANES, :] = jnp.concatenate(pieces, axis=0).T
+        body_rows = pl.ds(8, ROWS - 16)
+        copy = pltpu.make_async_copy(stage.at[k, body_rows], outs[k].at[body_rows], sems.at[k])
+        copy.start()
+        copies.append(copy)
 
     ones = jnp.ones((8, LANES), F32)
     for field in range(6):
@@ -484,97 +573,56 @@
         return rows[field, pl.ds(j, 8, stride=wide), :]
 
     zone.prepare(
-        row_tile,
+        0,
         load_row,
         lambda c: ((c == 31) & (group == 0)) | ((c == 63) & (group == 3)) | (c == BAND - 1),
         lambda c: jnp.where(
             (c < 32) & (group == 0), west, jnp.where((c >= 64) & (group == 3), east, spread)
         ),
     )
-    zone.begin(row_tile, load_row)
-    zone.prepare_north((row_tile,))
-
-    def start_of(step, side):
-        return STARTS[step] if side == 0 else WIDE - STRIP - STARTS[step]
-
-    for step in range(STEPS):
-        for side in range(2):
-            start = start_of(step, side)
-            for tile in range(2):
-                t = 2 * side + tile
-
-                def load(field, j):
-                    return ext[field, tile, pl.ds(start + j, 8, stride=size), :]
-
-                if step != 3:
-                    zone.prepare(
-                        t,
-                        load,
-                        lambda c: (c + start == HALO - 1)
-                        | (c + start == HALO + COLS - 1)
-                        | (c == STRIP - 1),
-                        lambda c: jnp.where(
-                            (c + start < HALO) if side == 0 else (c + start >= HALO + COLS),
-                            sides[side, tile],
-                            own_mask[tile],
-                        ),
-                    )
-                if step == 0:
-                    zone.begin(t, load)
-                else:
-                    for k in range(STATE):
-                        if side == 0:
-                            low, high = 8 * step, start + STRIP - HALO
-                        else:
-                            low, high = start - HALO, COLS - 8 * step
-                        plain[k, tile, HALO + low : HALO + high, :] = inner[
-                            step - 1, k, tile, low:high, :
-                        ]
-                        for j in range(size):
-                            zone.state[k][zone.base[t] + j] = plain[
-                                k, tile, pl.ds(start + j, 8, stride=size), :
-                            ]
-            if step != 3:
-                zone.prepare_north((2 * side, 2 * side + 1))
+    zone.begin(0, load_row)
+    zone.prepare_north((0,))
+
+    for _ in range(STEPS):
         zone.flows(pairs, drives)
         zone.rivers()
         zone.floods(pairs)
-        for side in range(2):
-            start = start_of(step, side)
-            for tile in range(2):
-                t = 2 * side + tile
-                for k in range(STATE):
-                    for j in range(size):
-                        plain[k, tile, pl.ds(start + j, 8, stride=size), :] = zone.state[k][
-                            zone.base[t] + j
-                        ]
 
     for k in range(4):
         for j in range(wide):
-            ends[k, pl.ds(j, 8, stride=wide), :] = zone.state[k][zone.base[row_tile] + j]
-    for k, target in enumerate((flood_out, river_out, east_out, north_out)):
-        for tile in range(2):
-            pieces = []
-            for i in range(COLS // 8):
-                if 3 <= i < 13:
-                    value = inner[STEPS - 1, k, tile, 8 * i : 8 * i + 8, :]
-                else:
-                    value = plain[k, tile, HALO + 8 * i : HALO + 8 * i + 8, :]
-                end = ends[k, 32 + 8 * (i % 4) : 40 + 8 * (i % 4), :]
-                shift = 32 * (i // 4)
-                if tile == 0:
-                    value = jnp.where(lane < 4, pltpu.roll(end, (104 - shift) % LANES, 1), value)
-                else:
-                    value = jnp.where(lane < 124, value, pltpu.roll(end, (120 - shift) % LANES, 1))
-                if k == LEVEL:
-                    at = HALO + 8 * i
-                    value = jnp.where(
-                        own_mask[tile] > 0.0,
-                        value - ext[BED, tile, at : at + 8, :],
-                        ext[RIVER, tile, at : at + 8, :],
-                    )
-                pieces.append(value)
-            target[tile * LANES : (tile + 1) * LANES, :] = jnp.concatenate(pieces, axis=0).T
+            ends[k, pl.ds(j, 8, stride=wide), :] = zone.state[k][zone.base[0] + j]
+    pieces = []
+    for k in range(4):
+        for at in range(32, 64, 8):
+            value = ends[k, at : at + 8, :]
+            if k == LEVEL:
+                value = jnp.where(
+                    spread > 0.0,
+                    value - rows[BED, at : at + 8, :],
+                    rows[RIVER, at : at + 8, :],
+                )
+            pieces.append(value)
+    turned = jnp.concatenate(pieces, axis=0).T
+    for k in range(4):
+        for which in range(2):
+            value = None
+            for g in range(4):
+                at = 32 * g + (24 if which == 0 else 0)
+                piece = turned[at : at + 8, :]
+                shift = (32 * g - 32 * k) % LANES
+                piece = pltpu.roll(piece, shift, 1) if shift else piece
+                value = piece if value is None else jnp.where(group == g, piece, value)
+            first = 0 if which == 0 else ROWS - 8
+            taken = (sublane < 4) if which == 0 else (sublane >= 4)
+            end_rows = pl.ds(first, 8)
+            stage[k, end_rows, :] = jnp.where(taken, value, stage[k, end_rows, :])
+            copy = pltpu.make_async_copy(
+                stage.at[k, end_rows], outs[k].at[end_rows], sems.at[4 + 2 * k + which]
+            )
+            copy.start()
+            copies.append(copy)
+    for copy in copies:
+        copy.wait()
 
 
 def body(n_lon, n_lat, depth_init, ground, roughness, river_init, reach_mask, width_class, bank_class):
@@ -592,9 +640,10 @@
             pltpu.VMEM((2, 8, LANES), F32),
             pltpu.VMEM((STEPS, STATE, 2, COLS, LANES), F32),
             pltpu.VMEM((6, BAND, LANES), F32),
+            pltpu.VMEM((STATE, 2, WIDE, LANES), F32),
         ),
         in_specs=[far] * 7,
-        out_specs=(near,) * 6,
+        out_specs=(near,) * 7,
         scratch_shapes=[
             pltpu.VMEM((4, ROWS, COLS), F32),
             pltpu.VMEM((2, ROWS, COLS), jnp.int32),
@@ -618,12 +667,13 @@
     return pl.pallas_call(
         functools.partial(flow_kernel, n_lat),
         out_shape=(jax.ShapeDtypeStruct(field, F32),) * 4,
-        in_specs=[near] * 6,
-        out_specs=(near,) * 4,
+        in_specs=[near] * 7,
+        out_specs=(far,) * 4,
         scratch_shapes=[
             pltpu.VMEM((6, BAND, LANES), F32),
-            pltpu.VMEM((STATE, 2, WIDE, LANES), F32),
             pltpu.VMEM((4, BAND, LANES), F32),
+            pltpu.VMEM((4, ROWS, COLS), F32),
+            pltpu.SemaphoreType.DMA((12,)),
         ]
         + state,
         compiler_params=pltpu.CompilerParams(vmem_limit_bytes=VMEM_LIMIT),

time: 36.7 us -> 37.5 us (1.022)
  Pallas kernels: 35.9 us -> 36.7 us
    pallas_call x1, Pallas kernels: 28.3 us -> 31.8 us  [body(): pl.pallas_call(functools.partial(exchange_kernel, n_lon, n_lat), out_shap...]
    pallas_call x1, Pallas kernels: 7.55 us -> 4.92 us  [body(): pl.pallas_call(functools.partial(flow_kernel, n_lat), out_shape=(jax.Shap...]
where the time goes in v3:
time: 37.5 us; the launch traced here: 37.4 us
  Pallas kernels  36.7 us (98%)
  between operations  0.64 us (2%)
    pallas_call x1, Pallas kernels, body(): pl.pallas_call(functools.partial(exchange_kernel, n_lon, n_lat), out_shap...  31.8 us
    pallas_call x1, Pallas kernels, body(): pl.pallas_call(functools.partial(flow_kernel, n_lat), out_shape=(jax.Shap...  4.92 us

profile of v3, /device:TPU:14, one launch (start us, length us, event | category | flops | bytes accessed | tf_op | source)
XLA Modules:
  0.0 37.4 jit_solution(1265776214856800922)
XLA Ops:
  0.6 31.8 %exchange.1 = (f32[6,2,176,128]{3,2,1,0:T(8,128)S(1)}, f32[2,2,8,128]{3,2,1,0:T(8,128)S(1)}, f32[6,7,8,128]{3,2,1,0:T(8,128)S(1)}, f32[2,8,128]{2,1,0:T(8,128)S(...) custom-call(f32[256,128]{1,0:T(8,128)} %depth_hbm.1, ...), custom_call_target="tpu_custom_call" | custom-call | tf_op jit(solution)/shard_map/exchange/pallas_call | solution.py:634
  32.5 4.9 %flow.1 = (f32[256,128]{1,0:T(8,128)}, f32[256,128]{1,0:T(8,128)}, f32[256,128]{1,0:T(8,128)}, f32[256,128]{1,0:T(8,128)}) custom-call(f32[6,2,176,128]{3,2,1,0:T(8,128)S(1)} %get-tuple-element.11.ext, f32[2,2,8,128]{3,2,1,0:T(8,128)S(1)} %get-tuple-element.12.sides, f32[6,7,8,128]{3,2,1,0:T(8,128)S(1)} %get-tuple-element.13.strips, ...), custom_call_target="tpu_custom_call" | custom-call | tf_op jit(solution)/shard_map/flow/pallas_call | solution.py:667

commit v4 on v3

--- a/solution.py
+++ b/solution.py
@@ -17,11 +17,10 @@
 HALO = 24
 WIDE = COLS + 2 * HALO
 LANES = 128
-STRIPS = (32, 32, 32, 40)
+STRIPS = (32, 40)
 BAND = 96
-STARTS = (0, 8, 16, 16)
 DEPTH, GROUND, ROUGH, RIVER, WIDTH, BED = range(6)
-FROM_S, FROM_N, FROM_SW, FROM_SE, FROM_NW, FROM_NE = range(6)
+FROM_S, FROM_N = range(2)
 FLOOD, LEVEL, EAST, NORTH, FLUX = range(5)
 
 GRAVITY = 9.81
@@ -245,6 +244,7 @@
     ext,
     sides,
     strips,
+    corners,
     own_mask,
     inner,
     band,
@@ -254,6 +254,7 @@
     mask_in,
     top,
     bottom,
+    packed,
     load_sem,
     send_sem,
     recv_sem,
@@ -270,10 +271,6 @@
         (west, lat),
         (lon, north),
         (lon, south),
-        (east, north),
-        (west, north),
-        (east, south),
-        (west, south),
     ]
     around = [{"lon": a, "lat": b} for a, b in around]
     barrier = pltpu.get_barrier_semaphore()
@@ -335,17 +332,15 @@
             ext.at[fields, both, pl.ds(HALO + COLS, HALO), :],
             around[1],
         ),
-        (bottom, strips.at[FROM_SW], around[4]),
-        (bottom, strips.at[FROM_SE], around[5]),
-        (top, strips.at[FROM_NW], around[6]),
-        (top, strips.at[FROM_NE], around[7]),
         (bottom, strips.at[FROM_S], around[2]),
         (top, strips.at[FROM_N], around[3]),
         (own_mask, sides.at[0], around[0]),
         (own_mask, sides.at[1], around[1]),
     ]
     copies = []
-    for number, (source, target, device) in enumerate(sends):
+
+    def send(source, target, device):
+        number = len(copies)
         copy = pltpu.make_async_remote_copy(
             src_ref=source,
             dst_ref=target,
@@ -356,6 +351,9 @@
         )
         copy.start()
         copies.append(copy)
+
+    for source, target, device in sends:
+        send(source, target, device)
 
     size = COLS // 8
     zone = Zone(scratch, [size, size], [1, 0])
@@ -400,16 +398,42 @@
                     value = jnp.where(zone.lane // 32 == k, moved, value)
             band[field, 8 * i : 8 * i + 8, :] = value
 
-    side_copies = (0, 1, 8, 9)
+    side_copies = (0, 1, 4, 5)
     for number in side_copies:
         copies[number].wait()
-    for step in range(STEPS):
-        strip = STRIPS[step]
+    sixteen = zone.lane // 16
+    for side in range(2):
+        for i in range(HALO // 8):
+            at = 8 * i + (HALO + COLS) * side
+            upper = pltpu.roll(sides[side, 0], 96, 1)
+            lower = pltpu.roll(sides[side, 1], 112, 1)
+            for field in range(6):
+                moved = ext[field, 0, at : at + 8, :]
+                moved = pltpu.roll(moved, 16 * field, 1) if field else moved
+                upper = jnp.where(sixteen == field, moved, upper)
+                moved = pltpu.roll(ext[field, 1, at : at + 8, :], 16 * field + 16, 1)
+                lower = jnp.where(sixteen == field, moved, lower)
+            packed[0, HALO * side + 8 * i : HALO * side + 8 * i + 8, :] = upper
+            packed[1, HALO * side + 8 * i : HALO * side + 8 * i + 8, :] = lower
+    send(packed.at[1], corners.at[FROM_S], around[2])
+    send(packed.at[0], corners.at[FROM_N], around[3])
+
+    zero = jnp.zeros((STRIPS[0], LANES), F32)
+    for side in range(2):
+        at = pl.ds((WIDE - STRIPS[0]) * side, STRIPS[0])
+        for tile in range(2):
+            plain[FLOOD, tile, at, :] = ext[DEPTH, tile, at, :]
+            plain[LEVEL, tile, at, :] = ext[BED, tile, at, :] + ext[RIVER, tile, at, :]
+            for k in (EAST, NORTH, FLUX):
+                plain[k, tile, at, :] = zero
+
+    def strip_step(step, shift, strip):
         size = strip // 8
         zone = Zone(scratch, [size] * 4, [1, 0, 3, 2])
         pairs = [(0, 1), (2, 3)]
+        starts = (shift, WIDE - strip - shift)
         for side in range(2):
-            start = start_of(step, side)
+            start = starts[side]
             for tile in range(2):
                 t = 2 * side + tile
 
@@ -428,22 +452,7 @@
                         own_mask[tile],
                     ),
                 )
-                if step == 0:
-                    zone.begin(t, load)
-                    continue
                 for k in range(STATE):
-                    if side == 0:
-                        low, high = 8 * (step - 1), start + strip - HALO
-                        edge, kept = low, zone.sublane == 0
-                    else:
-                        low, high = start - HALO, COLS - 8 * (step - 1)
-                        edge, kept = high - 8, zone.sublane == 7
-                    for at in range(low, high, 8):
-                        value = inner[step - 1, k, tile, at : at + 8, :]
-                        if step == 1 and at == edge and k in (FLOOD, EAST):
-                            old = plain[k, tile, HALO + at : HALO + at + 8, :]
-                            value = jnp.where(kept, old, value)
-                        plain[k, tile, HALO + at : HALO + at + 8, :] = value
                     for j in range(size):
                         zone.state[k][zone.base[t] + j] = plain[
                             k, tile, pl.ds(start + j, 8, stride=size), :
@@ -452,22 +461,38 @@
         zone.flows(pairs, [drives[0], drives[1], drives[0], drives[1]])
         zone.rivers()
         zone.floods(pairs)
+        last = strip != STRIPS[0]
         for side in range(2):
-            start = start_of(step, side)
+            start = starts[side]
             for tile in range(2):
                 t = 2 * side + tile
-                for k in range(STATE if step < STEPS - 1 else 4):
+                for k in range(4 if last else STATE):
                     for j in range(size):
                         plain[k, tile, pl.ds(start + j, 8, stride=size), :] = zone.state[k][
                             zone.base[t] + j
                         ]
+                    if last:
+                        continue
+                    for part in range(2):
+                        at = pl.multiple_of(
+                            8 * step + 8 * part if side == 0 else 112 - 8 * step + 8 * part, 8
+                        )
+                        value = inner[step, k, tile, pl.ds(at, 8), :]
+                        if part == side and k in (FLOOD, EAST):
+                            old = plain[k, tile, pl.ds(HALO + at, 8), :]
+                            kept = (zone.sublane == (7 if side else 0)) & (step == 0)
+                            value = jnp.where(kept, old, value)
+                        plain[k, tile, pl.ds(HALO + at, 8), :] = value
+
+    def early_step(step, carry):
+        strip_step(step, 8 * step, STRIPS[0])
+        return carry
+
+    lax.fori_loop(0, STEPS - 1, early_step, 0)
+    strip_step(STEPS - 1, 16, STRIPS[1])
     for number, copy in enumerate(copies):
         if number not in side_copies:
             copy.wait()
-
-
-def start_of(step, side):
-    return STARTS[step] if side == 0 else WIDE - STRIPS[step] - STARTS[step]
 
 
 def flow_kernel(
@@ -475,6 +500,7 @@
     ext,
     sides,
     strips,
+    corners,
     own_mask,
     inner,
     band,
@@ -524,46 +550,54 @@
         copies.append(copy)
 
     ones = jnp.ones((8, LANES), F32)
+    joined = [
+        jnp.where(
+            lane % 16 < 8,
+            corners[FROM_N, 8 * i : 8 * i + 8, :],
+            corners[FROM_S, 8 * i : 8 * i + 8, :],
+        )
+        for i in range(2 * HALO // 8)
+    ]
     for field in range(6):
         pieces = []
         for k in range(4):
             pieces.append(ones)
-            for west, middle, east in (
-                (FROM_NW, FROM_N, FROM_NE),
-                (FROM_SW, FROM_S, FROM_SE),
-            ):
-                value = strips[middle, field]
+            for which in (FROM_N, FROM_S):
+                value = strips[which, field]
                 if k != 1:
                     value = pltpu.roll(value, (160 - 32 * k) % LANES, 1)
-                if k == 0:
-                    value = jnp.where(lane < 32, pltpu.roll(strips[west, field], 32, 1), value)
-                if k == 3:
-                    value = jnp.where(lane < 64, value, pltpu.roll(strips[east, field], 64, 1))
                 pieces.append(value)
             pieces.append(ones)
         block = jnp.concatenate(pieces, axis=0).T
         for i in range(wide):
             value = band[field, 8 * i : 8 * i + 8, :]
-            if 1 <= i < 4:
-                at = 8 * (i - 1)
-                moved = fold(ext[field, 0, at : at + 8, :], ext[field, 1, at : at + 8, :])
-                value = jnp.where(group == 0, pltpu.roll(moved, 8, 1), value)
-            if 8 <= i < 11:
-                at = HALO + COLS + 8 * (i - 8)
-                moved = fold(ext[field, 0, at : at + 8, :], ext[field, 1, at : at + 8, :])
-                value = jnp.where(group == 3, pltpu.roll(moved, 104, 1), value)
-            rows[field, 8 * i : 8 * i + 8, :] = jnp.where(
-                halo_lane, block[8 * i : 8 * i + 8, :], value
-            )
-
-    def row_mask(low, high, north, south):
+            halo = block[8 * i : 8 * i + 8, :]
+            for side, first in ((0, 1), (1, 8)):
+                if first <= i < first + 3:
+                    ours = group == 3 * side
+                    at = 8 * (i - first)
+                    moved = pltpu.roll(
+                        joined[i - first + 3 * side], (8 + 96 * side - 16 * field) % LANES, 1
+                    )
+                    halo = jnp.where(ours, moved, halo)
+                    at += (HALO + COLS) * side
+                    moved = fold(ext[field, 0, at : at + 8, :], ext[field, 1, at : at + 8, :])
+                    value = jnp.where(ours, pltpu.roll(moved, 8 + 96 * side, 1), value)
+            rows[field, 8 * i : 8 * i + 8, :] = jnp.where(halo_lane, halo, value)
+
+    def row_mask(low, high, halo):
         value = jnp.where(place < 8, pltpu.roll(high, 8, 1), pltpu.roll(low, 24, 1))
-        value = jnp.where(halo_lane & (place < 16), pltpu.roll(north, 8, 1), value)
-        return jnp.where(halo_lane & (place >= 16), pltpu.roll(south, 24, 1), value)
-
-    middle = row_mask(own_mask[0], own_mask[1], strips[FROM_N, 6], strips[FROM_S, 6])
-    west = row_mask(sides[0, 0], sides[0, 1], strips[FROM_NW, 6], strips[FROM_SW, 6])
-    east = row_mask(sides[1, 0], sides[1, 1], strips[FROM_NE, 6], strips[FROM_SE, 6])
+        return jnp.where(halo_lane, halo, value)
+
+    middle = row_mask(
+        own_mask[0],
+        own_mask[1],
+        jnp.where(
+            place < 16, pltpu.roll(strips[FROM_N, 6], 8, 1), pltpu.roll(strips[FROM_S, 6], 24, 1)
+        ),
+    )
+    west = row_mask(sides[0, 0], sides[0, 1], pltpu.roll(joined[0], 40, 1))
+    east = row_mask(sides[1, 0], sides[1, 1], pltpu.roll(joined[3], 40, 1))
     east = pltpu.roll(east, 96, 1)
     spread = middle
     for k in range(1, 4):
@@ -583,10 +617,13 @@
     zone.begin(0, load_row)
     zone.prepare_north((0,))
 
-    for _ in range(STEPS):
+    def step(_, carry):
         zone.flows(pairs, drives)
         zone.rivers()
         zone.floods(pairs)
+        return carry
+
+    lax.fori_loop(0, STEPS, step, 0)
 
     for k in range(4):
         for j in range(wide):
@@ -636,23 +673,25 @@
         out_shape=(
             pltpu.VMEM((6, 2, WIDE, LANES), F32),
             pltpu.VMEM((2, 2, 8, LANES), F32),
-            pltpu.VMEM((6, 7, 8, LANES), F32),
+            pltpu.VMEM((2, 7, 8, LANES), F32),
+            pltpu.VMEM((2, 2 * HALO, LANES), F32),
             pltpu.VMEM((2, 8, LANES), F32),
             pltpu.VMEM((STEPS, STATE, 2, COLS, LANES), F32),
             pltpu.VMEM((6, BAND, LANES), F32),
             pltpu.VMEM((STATE, 2, WIDE, LANES), F32),
         ),
         in_specs=[far] * 7,
-        out_specs=(near,) * 7,
+        out_specs=(near,) * 8,
         scratch_shapes=[
             pltpu.VMEM((4, ROWS, COLS), F32),
             pltpu.VMEM((2, ROWS, COLS), jnp.int32),
             pltpu.VMEM((2, LANES), jnp.int32),
             pltpu.VMEM((7, 8, LANES), F32),
             pltpu.VMEM((7, 8, LANES), F32),
+            pltpu.VMEM((2, 2 * HALO, LANES), F32),
             pltpu.SemaphoreType.DMA((7,)),
-            pltpu.SemaphoreType.DMA((10,)),
-            pltpu.SemaphoreType.DMA((10,)),
+            pltpu.SemaphoreType.DMA((8,)),
+            pltpu.SemaphoreType.DMA((8,)),
         ]
         + state,
         compiler_params=pltpu.CompilerParams(
@@ -667,7 +706,7 @@
     return pl.pallas_call(
         functools.partial(flow_kernel, n_lat),
         out_shape=(jax.ShapeDtypeStruct(field, F32),) * 4,
-        in_specs=[near] * 7,
+        in_specs=[near] * 8,
         out_specs=(far,) * 4,
         scratch_shapes=[
             pltpu.VMEM((6, BAND, LANES), F32),

time: 37.5 us -> 36.3 us (0.968)
  Pallas kernels: 36.7 us -> 35.5 us
    pallas_call x1, Pallas kernels: 31.8 us -> 30.4 us  [body(): pl.pallas_call(functools.partial(exchange_kernel, n_lon, n_lat), out_shap...]
where the time goes in v4:
time: 36.3 us; the launch traced here: 36.1 us
  Pallas kernels  35.5 us (98%)
  between operations  0.64 us (2%)
    pallas_call x1, Pallas kernels, body(): pl.pallas_call(functools.partial(exchange_kernel, n_lon, n_lat), out_shap...  30.4 us
    pallas_call x1, Pallas kernels, body(): pl.pallas_call(functools.partial(flow_kernel, n_lat), out_shape=(jax.Shap...  5.06 us

profile of v4, /device:TPU:14, one launch (start us, length us, event | category | flops | bytes accessed | tf_op | source)
XLA Modules:
  0.0 36.1 jit_solution(8216281565307593859)
XLA Ops:
  0.6 30.4 %exchange.1 = (f32[6,2,176,128]{3,2,1,0:T(8,128)S(1)}, f32[2,2,8,128]{3,2,1,0:T(8,128)S(1)}, f32[2,7,8,128]{3,2,1,0:T(8,128)S(1)}, f32[2,48,128]{2,1,0:T(8,128)S...) custom-call(f32[256,128]{1,0:T(8,128)} %depth_hbm.1, ...), custom_call_target="tpu_custom_call" | custom-call | tf_op jit(solution)/shard_map/exchange/pallas_call | solution.py:671
  31.1 5.1 %flow.1 = (f32[256,128]{1,0:T(8,128)}, f32[256,128]{1,0:T(8,128)}, f32[256,128]{1,0:T(8,128)}, f32[256,128]{1,0:T(8,128)}) custom-call(f32[6,2,176,128]{3,2,1,0:T(8,128)S(1)} %get-tuple-element.12.ext, f32[2,2,8,128]{3,2,1,0:T(8,128)S(1)} %get-tuple-element.13.sides, f32[2,7,8,128]{3,2,1,0:T(8,128)S(1)} %get-tuple-element.14.strips, ...), custom_call_target="tpu_custom_call" | custom-call | tf_op jit(solution)/shard_map/flow/pallas_call | solution.py:706

commit v5 on v4

--- a/solution.py
+++ b/solution.py
@@ -36,6 +36,7 @@
 STATE = 5
 SCRATCH = 17
 REGISTERS = 32
+UNROLL = 8
 VMEM_LIMIT = 24 << 20
 
 
@@ -170,6 +171,49 @@
                     )
 
     def rivers(self):
+        level, flux = self.state[LEVEL], self.state[FLUX]
+        rate = SHORT_STEP * EXCHANGE
+
+        if sum(self.sizes) > 20:
+            return self.rivers_in_memory()
+        count = sum(self.sizes)
+
+        def substep(_, carry):
+            levels, fluxes = list(carry[:count]), list(carry[count:])
+            outs = [None] * count
+            for t, size in enumerate(self.sizes):
+                base = self.base[t]
+                for j in range(size):
+                    at = base + j
+                    here = levels[at]
+                    there = levels[at + 1] if j + 1 < size else pltpu.roll(levels[base], 7, 0)
+                    outs[at] = quotient(
+                        fluxes[at],
+                        jnp.maximum(here, there) - self.r_base[at],
+                        there - here,
+                        self.r_fric[at],
+                        self.r_drive[at],
+                    )
+                    self.total[at] += here
+            fresh = []
+            for t, size in enumerate(self.sizes):
+                base = self.base[t]
+                for j in range(size):
+                    at = base + j
+                    west = outs[at - 1] if j else pltpu.roll(outs[base + size - 1], 1, 0)
+                    fresh.append(
+                        (1.0 - rate) * levels[at]
+                        + (rate * self.sur[at] + (west - outs[at]) * self.r_inv[at])
+                    )
+            return tuple(fresh) + tuple(outs)
+
+        start = [level[at] for at in range(count)] + [flux[at] for at in range(count)]
+        final = lax.fori_loop(0, SUB, substep, tuple(start), unroll=UNROLL)
+        for at in range(count):
+            level[at] = final[at]
+            flux[at] = final[count + at]
+
+    def rivers_in_memory(self):
         level, flux = self.state[LEVEL], self.state[FLUX]
         rate = SHORT_STEP * EXCHANGE
 
@@ -484,11 +528,8 @@
                             value = jnp.where(kept, old, value)
                         plain[k, tile, pl.ds(HALO + at, 8), :] = value
 
-    def early_step(step, carry):
+    for step in range(STEPS - 1):
         strip_step(step, 8 * step, STRIPS[0])
-        return carry
-
-    lax.fori_loop(0, STEPS - 1, early_step, 0)
     strip_step(STEPS - 1, 16, STRIPS[1])
     for number, copy in enumerate(copies):
         if number not in side_copies:
@@ -623,7 +664,8 @@
         zone.floods(pairs)
         return carry
 
-    lax.fori_loop(0, STEPS, step, 0)
+    for _ in range(STEPS):
+        step(_, 0)
 
     for k in range(4):
         for j in range(wide):

time: 36.3 us -> 34.3 us (0.945)
  Pallas kernels: 35.5 us -> 33.5 us
    pallas_call x1, Pallas kernels: 5.06 us -> 3.05 us  [body(): pl.pallas_call(functools.partial(flow_kernel, n_lat), out_shape=(jax.Shap...]
where the time goes in v5:
time: 34.3 us; the launch traced here: 34.1 us
  Pallas kernels  33.5 us (98%)
  between operations  0.64 us (2%)
    pallas_call x1, Pallas kernels, body(): pl.pallas_call(functools.partial(exchange_kernel, n_lon, n_lat), out_shap...  30.4 us
    pallas_call x1, Pallas kernels, body(): pl.pallas_call(functools.partial(flow_kernel, n_lat), out_shape=(jax.Shap...  3.05 us

profile of v5, /device:TPU:14, one launch (start us, length us, event | category | flops | bytes accessed | tf_op | source)
XLA Modules:
  0.0 34.1 jit_solution(16407666065994712235)
XLA Ops:
  0.6 30.4 %exchange.1 = (f32[6,2,176,128]{3,2,1,0:T(8,128)S(1)}, f32[2,2,8,128]{3,2,1,0:T(8,128)S(1)}, f32[2,7,8,128]{3,2,1,0:T(8,128)S(1)}, f32[2,48,128]{2,1,0:T(8,128)S...) custom-call(f32[256,128]{1,0:T(8,128)} %depth_hbm.1, ...), custom_call_target="tpu_custom_call" | custom-call | tf_op jit(solution)/shard_map/exchange/pallas_call | solution.py:713
  31.1 3.1 %flow.1 = (f32[256,128]{1,0:T(8,128)}, f32[256,128]{1,0:T(8,128)}, f32[256,128]{1,0:T(8,128)}, f32[256,128]{1,0:T(8,128)}) custom-call(f32[6,2,176,128]{3,2,1,0:T(8,128)S(1)} %get-tuple-element.12.ext, f32[2,2,8,128]{3,2,1,0:T(8,128)S(1)} %get-tuple-element.13.sides, f32[2,7,8,128]{3,2,1,0:T(8,128)S(1)} %get-tuple-element.14.strips, ...), custom_call_target="tpu_custom_call" | custom-call | tf_op jit(solution)/shard_map/flow/pallas_call | solution.py:748

commit v6 on v5

--- a/solution.py
+++ b/solution.py
@@ -299,6 +299,7 @@
     top,
     bottom,
     packed,
+    relay,
     load_sem,
     send_sem,
     recv_sem,
@@ -361,11 +362,28 @@
         own_mask[tile] = jnp.broadcast_to(mask_in[tile : tile + 1, :].astype(F32), (8, LANES))
     top[6] = own_mask[0]
     bottom[6] = own_mask[1]
+    sixteen = lax.broadcasted_iota(jnp.int32, (8, LANES), 1) // 16
+    upper_mask = pltpu.roll(own_mask[0], 96, 1)
+    lower_mask = pltpu.roll(own_mask[1], 112, 1)
+    for side in range(2):
+        for i in range(HALO // 8):
+            at = 8 * i + (COLS if side else HALO)
+            upper, lower = upper_mask, lower_mask
+            for field in range(6):
+                moved = ext[field, 0, at : at + 8, :]
+                moved = pltpu.roll(moved, 16 * field, 1) if field else moved
+                upper = jnp.where(sixteen == field, moved, upper)
+                moved = pltpu.roll(ext[field, 1, at : at + 8, :], 16 * field + 16, 1)
+                lower = jnp.where(sixteen == field, moved, lower)
+            packed[side, 0, 8 * i : 8 * i + 8, :] = upper
+            packed[side, 1, 8 * i : 8 * i + 8, :] = lower
 
     pl.semaphore_wait(barrier, len(around))
     fields = pl.ds(0, 6)
     both = pl.ds(0, 2)
     sends = [
+        (packed.at[1], relay.at[0], around[0]),
+        (packed.at[0], relay.at[1], around[1]),
         (
             ext.at[fields, both, pl.ds(COLS, HALO), :],
             ext.at[fields, both, pl.ds(0, HALO), :],
@@ -425,6 +443,12 @@
 
     lax.fori_loop(0, STEPS, step, 0)
 
+    for side in (1, 0):
+        copies[side].wait()
+        where = pl.ds(HALO * side, HALO)
+        send(relay.at[side, 1], corners.at[FROM_S, where], around[2])
+        send(relay.at[side, 0], corners.at[FROM_N, where], around[3])
+
     for field in range(6):
         values = [
             fold(
@@ -442,26 +466,8 @@
                     value = jnp.where(zone.lane // 32 == k, moved, value)
             band[field, 8 * i : 8 * i + 8, :] = value
 
-    side_copies = (0, 1, 4, 5)
-    for number in side_copies:
+    for number in (2, 3, 6, 7):
         copies[number].wait()
-    sixteen = zone.lane // 16
-    for side in range(2):
-        for i in range(HALO // 8):
-            at = 8 * i + (HALO + COLS) * side
-            upper = pltpu.roll(sides[side, 0], 96, 1)
-            lower = pltpu.roll(sides[side, 1], 112, 1)
-            for field in range(6):
-                moved = ext[field, 0, at : at + 8, :]
-                moved = pltpu.roll(moved, 16 * field, 1) if field else moved
-                upper = jnp.where(sixteen == field, moved, upper)
-                moved = pltpu.roll(ext[field, 1, at : at + 8, :], 16 * field + 16, 1)
-                lower = jnp.where(sixteen == field, moved, lower)
-            packed[0, HALO * side + 8 * i : HALO * side + 8 * i + 8, :] = upper
-            packed[1, HALO * side + 8 * i : HALO * side + 8 * i + 8, :] = lower
-    send(packed.at[1], corners.at[FROM_S], around[2])
-    send(packed.at[0], corners.at[FROM_N], around[3])
-
     zero = jnp.zeros((STRIPS[0], LANES), F32)
     for side in range(2):
         at = pl.ds((WIDE - STRIPS[0]) * side, STRIPS[0])
@@ -531,9 +537,8 @@
     for step in range(STEPS - 1):
         strip_step(step, 8 * step, STRIPS[0])
     strip_step(STEPS - 1, 16, STRIPS[1])
-    for number, copy in enumerate(copies):
-        if number not in side_copies:
-            copy.wait()
+    for number in (4, 5, 8, 9, 10, 11):
+        copies[number].wait()
 
 
 def flow_kernel(
@@ -730,10 +735,11 @@
             pltpu.VMEM((2, LANES), jnp.int32),
             pltpu.VMEM((7, 8, LANES), F32),
             pltpu.VMEM((7, 8, LANES), F32),
-            pltpu.VMEM((2, 2 * HALO, LANES), F32),
+            pltpu.VMEM((2, 2, HALO, LANES), F32),
+            pltpu.VMEM((2, 2, HALO, LANES), F32),
             pltpu.SemaphoreType.DMA((7,)),
-            pltpu.SemaphoreType.DMA((8,)),
-            pltpu.SemaphoreType.DMA((8,)),
+            pltpu.SemaphoreType.DMA((12,)),
+            pltpu.SemaphoreType.DMA((12,)),
         ]
         + state,
         compiler_params=pltpu.CompilerParams(

time: 34.3 us -> 33.6 us (0.980)
  Pallas kernels: 33.5 us -> 32.8 us
    pallas_call x1, Pallas kernels: 30.4 us -> 29.7 us  [body(): pl.pallas_call(functools.partial(exchange_kernel, n_lon, n_lat), out_shap...]
where the time goes in v6:
time: 33.6 us; the launch traced here: 33.4 us
  Pallas kernels  32.8 us (98%)
  between operations  0.64 us (2%)
    pallas_call x1, Pallas kernels, body(): pl.pallas_call(functools.partial(exchange_kernel, n_lon, n_lat), out_shap...  29.7 us
    pallas_call x1, Pallas kernels, body(): pl.pallas_call(functools.partial(flow_kernel, n_lat), out_shape=(jax.Shap...  3.05 us

profile of v6, /device:TPU:14, one launch (start us, length us, event | category | flops | bytes accessed | tf_op | source)
XLA Modules:
  0.0 33.4 jit_solution(4899749342059315962)
XLA Ops:
  0.6 29.7 %exchange.1 = (f32[6,2,176,128]{3,2,1,0:T(8,128)S(1)}, f32[2,2,8,128]{3,2,1,0:T(8,128)S(1)}, f32[2,7,8,128]{3,2,1,0:T(8,128)S(1)}, f32[2,48,128]{2,1,0:T(8,128)S...) custom-call(f32[256,128]{1,0:T(8,128)} %depth_hbm.1, ...), custom_call_target="tpu_custom_call" | custom-call | tf_op jit(solution)/shard_map/exchange/pallas_call | solution.py:718
  30.4 3.1 %flow.1 = (f32[256,128]{1,0:T(8,128)}, f32[256,128]{1,0:T(8,128)}, f32[256,128]{1,0:T(8,128)}, f32[256,128]{1,0:T(8,128)}) custom-call(f32[6,2,176,128]{3,2,1,0:T(8,128)S(1)} %get-tuple-element.12.ext, f32[2,2,8,128]{3,2,1,0:T(8,128)S(1)} %get-tuple-element.13.sides, f32[2,7,8,128]{3,2,1,0:T(8,128)S(1)} %get-tuple-element.14.strips, ...), custom_call_target="tpu_custom_call" | custom-call | tf_op jit(solution)/shard_map/flow/pallas_call | solution.py:754

commit v7 on v6

--- a/solution.py
+++ b/solution.py
@@ -253,7 +253,7 @@
                 )
             return carry
 
-        lax.fori_loop(0, SUB, substep, 0)
+        lax.fori_loop(0, SUB, substep, 0, unroll=2)
 
     def floods(self, pairs):
         flood, _, q_east, q_north, _ = self.state

time: 33.6 us -> 33.3 us (level)
  no operation moved by 1% of the time
where the time goes in v7:
time: 33.3 us; the launch traced here: 33.1 us
  Pallas kernels  32.5 us (98%)
  between operations  0.64 us (2%)
    pallas_call x1, Pallas kernels, body(): pl.pallas_call(functools.partial(exchange_kernel, n_lon, n_lat), out_shap...  29.4 us
    pallas_call x1, Pallas kernels, body(): pl.pallas_call(functools.partial(flow_kernel, n_lat), out_shape=(jax.Shap...  3.05 us

profile of v7, /device:TPU:14, one launch (start us, length us, event | category | flops | bytes accessed | tf_op | source)
XLA Modules:
  0.0 33.1 jit_solution(15408519944124766692)
XLA Ops:
  0.6 29.4 %exchange.1 = (f32[6,2,176,128]{3,2,1,0:T(8,128)S(1)}, f32[2,2,8,128]{3,2,1,0:T(8,128)S(1)}, f32[2,7,8,128]{3,2,1,0:T(8,128)S(1)}, f32[2,48,128]{2,1,0:T(8,128)S...) custom-call(f32[256,128]{1,0:T(8,128)} %depth_hbm.1, ...), custom_call_target="tpu_custom_call" | custom-call | tf_op jit(solution)/shard_map/exchange/pallas_call | solution.py:718
  30.1 3.1 %flow.1 = (f32[256,128]{1,0:T(8,128)}, f32[256,128]{1,0:T(8,128)}, f32[256,128]{1,0:T(8,128)}, f32[256,128]{1,0:T(8,128)}) custom-call(f32[6,2,176,128]{3,2,1,0:T(8,128)S(1)} %get-tuple-element.12.ext, f32[2,2,8,128]{3,2,1,0:T(8,128)S(1)} %get-tuple-element.13.sides, f32[2,7,8,128]{3,2,1,0:T(8,128)S(1)} %get-tuple-element.14.strips, ...), custom_call_target="tpu_custom_call" | custom-call | tf_op jit(solution)/shard_map/flow/pallas_call | solution.py:754
